TPU v7x, 256 devices: a whole 4x4x8 slice. The times are simulated.
256 devices in a mesh: grp: 4 (over z_hi, core), dev: 64 (over x, z_lo, y).
Axes of the slice: x: 4, y: 4, z: 8 (z_hi: 2, z_lo: 4; z = z_hi * 4 + z_lo), core: 2. Of those that a mesh axis runs over, the one named last changes fastest.
Arguments:
- tables: float32 [4, 524288, 128], P(None, ('grp', 'dev')), may hold values from -6 to 6
- accum: float32 [4, 524288], P(None, ('grp', 'dev')), may hold values from 0.01 to 10
- block_position: int32 [4, 4096], replicated, may hold values from 0 to 4095, as said below
- lookup_ids: int32 [65536, 4], P(('grp', 'dev')), may hold values from 0 to 524287, as said below
Outputs:
- new_tables: float32 [4, 524288, 128], P('grp', 'dev')
- new_accum: float32 [4, 524288], P('grp', 'dev')
- looked: float32 [65536, 4, 128], P(('grp', 'dev'))
Inputs may be any that keep to these rules, and one draw needn't show every extreme that they name: `block_position`: for each table a permutation of 0 to 4095. Old block b lies on the device b // 16 of grp+dev; call its dev index its source, and p // 64 the owner of new block p. For every table, source and owner, at most 2 blocks of that source go to that owner, and 2 is reached. `lookup_ids`: the owner of an id of table t is block_position[t, id // 128] // 64. Among one device's 256 rows, at most 8 ids of one table have one owner, and 8 is reached for every device and table.
All inputs are finite; a program needn't handle non-finite values.
Results may differ from a plain program's by a relative error of at most 0.00002.
Values sent between devices are 32-bit elements; how exact they have to be, the bound alone decides.
No kernel may reach another device: no remote copies, remote signals or barrier semaphores. Data moves between devices by JAX's collectives and lax.ppermute only.
A program may use at most 128 MiB of HBM per device.

v0:
```python
import jax
import jax.numpy as jnp
from jax import lax
from jax.sharding import PartitionSpec as P

TILE = 128


def shifted(shard, axis, by):
    peers = lax.axis_size(axis)
    return lax.ppermute(shard, axis, [(i, (i + by) % peers) for i in range(peers)])


def in_blocks(shard, dim, peers):
    shape = shard.shape
    pieces = shard.reshape(*shape[:dim], peers, shape[dim] // peers, *shape[dim + 1 :])
    return jnp.moveaxis(pieces, dim, 0)


def in_order(pieces, dim):
    pieces = jnp.moveaxis(pieces, 0, dim)
    shape = pieces.shape
    return pieces.reshape(*shape[:dim], shape[dim] * shape[dim + 1], *shape[dim + 2 :])


def joined_exchange(shard, axis, axes, splits, concats):
    sizes = [lax.axis_size(a) for a in axes]
    pieces = in_blocks(shard, splits[0], sizes[0])
    pieces = jnp.moveaxis(in_blocks(pieces, splits[1] + 1, sizes[1]), 0, 1)
    inside = pieces.shape[2:]
    pieces = pieces.reshape(-1, *inside)
    pieces = lax.all_to_all(pieces, axis, split_axis=0, concat_axis=0, tiled=True)
    pieces = in_order(pieces.reshape(*sizes, *inside), concats[0] + 1)
    return in_order(pieces, concats[1])


def body(tables, accum, block_position, lookup_ids):
    groups = lax.axis_size("grp")
    shards = lax.axis_size("dev")
    my_group = lax.axis_index("grp")
    my_shard = lax.axis_index("dev")
    table_count, old_rows, width = tables.shape
    tile_rows = TILE
    own_rows = lax.dynamic_index_in_dim(tables, my_group, 0, keepdims=False)
    own_sums = lax.dynamic_index_in_dim(accum, my_group, 0, keepdims=False)
    held = jnp.zeros((groups, old_rows, width), jnp.float32)
    held_sums = jnp.zeros((groups, old_rows), jnp.float32)
    held = lax.dynamic_update_index_in_dim(held, own_rows, my_group, 0)
    held_sums = lax.dynamic_update_index_in_dim(held_sums, own_sums, my_group, 0)
    for step_by in range(1, groups):
        wanted = (my_group + step_by) % groups
        send_rows = lax.dynamic_index_in_dim(tables, wanted, 0, keepdims=False)
        send_sums = lax.dynamic_index_in_dim(accum, wanted, 0, keepdims=False)
        got_rows, got_sums = shifted((send_rows, send_sums), "grp", step_by)
        anchor = (my_group - step_by) % groups
        held = lax.dynamic_update_index_in_dim(held, got_rows, anchor, 0)
        held_sums = lax.dynamic_update_index_in_dim(held_sums, got_sums, anchor, 0)
    blocks = held.reshape(groups * old_rows // tile_rows, tile_rows, width)
    block_sums = held_sums.reshape(groups * old_rows // tile_rows, tile_rows)
    local = blocks.shape[0]
    per_old = old_rows // tile_rows
    counter = jnp.arange(local, dtype=jnp.int32)
    old_index = (counter // per_old * shards + my_shard) * per_old + counter % per_old
    position_row = lax.dynamic_index_in_dim(block_position, my_group, 0, keepdims=False)
    new_place = position_row[old_index]
    target = new_place // local
    slot_place = new_place % local
    longer = local // 2 + 1
    capacity = -(-longer // shards) + -(-(local - longer) // shards)
    marks = (target[:, None] == jnp.arange(shards, dtype=jnp.int32)[None, :]).astype(jnp.int32)
    order_in = jnp.sum((jnp.cumsum(marks, axis=0) - marks) * marks, axis=1)
    slot_index = target * capacity + order_in
    source_of = jnp.zeros((shards * capacity,), jnp.int32).at[slot_index].set(counter)
    filled = jnp.zeros((shards * capacity,), jnp.int32).at[slot_index].set(1)
    weight = filled.astype(jnp.float32)
    send_blocks = (blocks[source_of] * weight[:, None, None]).reshape(
        shards, capacity, tile_rows, width
    )
    send_sums = (block_sums[source_of] * weight[:, None]).reshape(shards, capacity, tile_rows)
    send_place = jnp.where(filled == 1, slot_place[source_of], -1).reshape(shards, capacity)
    got_blocks, got_sums, got_place = (
        lax.all_to_all(send_blocks, "dev", split_axis=0, concat_axis=0, tiled=True),
        lax.all_to_all(send_sums, "dev", split_axis=0, concat_axis=0, tiled=True),
        lax.all_to_all(send_place, "dev", split_axis=0, concat_axis=0, tiled=True),
    )
    flat_place = got_place.reshape(-1)
    landing = jnp.where(flat_place >= 0, flat_place, local)
    picker = (
        jnp.zeros((local,), jnp.int32)
        .at[landing]
        .set(jnp.arange(shards * capacity, dtype=jnp.int32), mode="drop")
    )
    new_blocks = got_blocks.reshape(shards * capacity, tile_rows, width)[picker]
    new_sums = got_sums.reshape(shards * capacity, tile_rows)[picker]
    rows_here = local * tile_rows
    new_table = new_blocks.reshape(1, rows_here, width)
    new_accum = new_sums.reshape(1, rows_here)
    look_rows = lookup_ids.shape[0]
    limit = 2 * look_rows // shards
    table_ids = jnp.arange(table_count, dtype=jnp.int32)[None, :]
    id_place = block_position[table_ids, lookup_ids // tile_rows]
    owner = id_place // local
    local_row = id_place % local * tile_rows + lookup_ids % tile_rows
    owner_marks = (owner[..., None] == jnp.arange(shards, dtype=jnp.int32)[None, None, :]).astype(
        jnp.int32
    )
    owner_order = jnp.sum((jnp.cumsum(owner_marks, axis=0) - owner_marks) * owner_marks, axis=2)
    table_grid = jnp.broadcast_to(table_ids, owner.shape)
    asking = (
        jnp.full((table_count, shards, limit), -1, jnp.int32)
        .at[table_grid, owner, owner_order]
        .set(local_row)
    )
    asked = joined_exchange(asking, ("grp", "dev"), ("grp", "dev"), (0, 1), (0, 1))
    wanted_rows = asked.reshape(-1)
    answer = new_blocks.reshape(rows_here, width)[jnp.maximum(wanted_rows, 0)]
    returned = joined_exchange(
        answer.reshape(groups, shards, limit, width), ("grp", "dev"), ("grp", "dev"), (0, 1), (0, 1)
    )
    looked = returned[table_grid, owner, owner_order]
    return (new_table, new_accum, looked)


def solution(mesh):
    placed = (P(None, ("grp", "dev"), None), P(None, ("grp", "dev")), P(), P(("grp", "dev"), None))
    return jax.shard_map(
        body,
        mesh=mesh,
        in_specs=placed,
        out_specs=(P("grp", "dev", None), P("grp", "dev"), P(("grp", "dev"), None, None)),
        check_vma=False,
    )
```

profile of v0, /device:TPU:1, one launch (start us, length us, event | category | flops | bytes accessed | tf_op | source)
XLA Modules:
  0.0 419.1 jit_solution(9096033704801920639)
XLA Ops:
  0.7 2.4 broadcast_in_dim.77
  6.0 8.3 %collective-permute-start = (f32[2048,128]{1,0:T(8,128)}, f32[2048,128]{1,0:T(8,128)}, u32[]{:S(2)}, u32[]{:S(2)}) collective-permute-start(f32[2048,128]{1,0:T(8,128)} %get-tuple-element.6), channel_id=1, source_target_pairs={{0,64},{64,128},{128,192},{192,0},{1,65},{65,129},{129,193},{193,1... | collective-permute-start | bytes 3145736 | tf_op jit(solution)/shard_map/ppermute | solution.py:11
  19.5 9.8 %all-to-all-start.1 = ((s32[64,1,2]{2,1,0:T(1,128)}), s32[64,1,2]{2,1,0:T(1,128)S(1)}, u32[]{:S(2)}, u32[]{:S(2)}) async-start(s32[64,1,2]{2,1,0:T(1,128)} %bitcast.14), calls=%async_computation.1 | async-start | bytes 65536 | tf_op jit(solution)/shard_map/all_to_all | solution.py:84
  29.6 9.1 %gather_fusion.6 = s32[1024]{0:T(1024)S(1)} fusion(s32[4,4096]{1,0:T(4,128)S(1)} %copy-done, s32[1024]{0:T(1024)S(1)} %reshape.406), kind=kCustom, calls=%fused_computation.6 | custom fusion | bytes 16384 | tf_op jit(solution)/shard_map/gather | solution.py:101
  39.1 2.4 reduce-window.6
  43.3 4.3 %scatter_custom_fusion.3 = s32[2048]{0:T(1024)S(1)} fusion(s32[1024]{0:T(1024)S(1)} %reshape.450, s32[1024]{0:T(1024)S(1)} %reshape.452, s32[]{:T(128)} %constant.205.clone.1), kind=kCustom, calls=%fused_computation.76 | custom fusion | bytes 8196
  50.7 24.3 %collective-permute-done.1 = f32[2048,128]{1,0:T(8,128)} collective-permute-done((f32[2048,128]{1,0:T(8,128)S(1)}, f32[2048,128]{1,0:T(8,128)}, u32[]{:S(2)}, u32[]{:S(2)}) %collective-permute-start.1) | collective-permute-done | bytes 1048608 | tf_op jit(solution)/shard_map/ppermute | solution.py:11
  77.3 2.3 bitcast_dynamic-update-slice_fusion
  79.5 6.5 %gather_fusion.1 = f32[128,128,128]{2,1,0:T(8,128)} fusion(f32[64,128,128]{2,1,0:T(8,128)} %bitcast.6, s32[1024]{0:T(1024)S(1)} %pad_clamp_fusion.1), kind=kCustom, calls=%fused_computation.1 | custom fusion | bytes 16777728 | tf_op jit(solution)/shard_map/gather | solution.py:76
  86.0 25.4 %all-to-all-done.1 = s32[64,1,2]{2,1,0:T(1,128)S(1)} async-done(((s32[64,1,2]{2,1,0:T(1,128)}), s32[64,1,2]{2,1,0:T(1,128)S(1)}, u32[]{:S(2)}, u32[]{:S(2)}) %all-to-all-start.1) | async-done | bytes 544 | tf_op jit(solution)/shard_map/all_to_all | solution.py:84
  111.5 17.7 %all-to-all-start.3 = ((s32[256,1,1,8]{3,2,1,0:T(1,128)}), s32[256,1,1,8]{3,2,1,0:T(1,128)S(1)}, u32[]{:S(2)}, u32[]{:S(2)}) async-start(s32[256,1,1,8]{3,2,1,0:T(1,128)} %bitcast.33), calls=%async_computation.3 | async-start | bytes 262144 | tf_op jit(solution)/shard_map/all_to_all | solution.py:32
  129.2 7.2 %broadcast_multiply_fusion = f32[64,2,128,128]{3,2,1,0:T(8,128)} fusion(f32[64,2,128,128]{3,2,1,0:T(8,128)} %bitcast.123, f32[64,2]{1,0:T(8,128)S(1)} %mul.73), kind=kLoop, calls=%fused_computation.13 | loop fusion | flops 2097152 | bytes 16777728 | tf_op jit(solution)/shard_map/mul | solution.py:76
  136.4 5.7 %all-to-all-done.3 = s32[256,1,1,8]{3,2,1,0:T(1,128)S(1)} async-done(((s32[256,1,1,8]{3,2,1,0:T(1,128)}), s32[256,1,1,8]{3,2,1,0:T(1,128)S(1)}, u32[]{:S(2)}, u32[]{:S(2)}) %all-to-all-start.3) | async-done | bytes 8224 | tf_op jit(solution)/shard_map/all_to_all | solution.py:32
  142.1 6.0 %all-to-all-start = ((f32[64,2,128,128]{3,2,1,0:T(8,128)}), f32[64,2,128,128]{3,2,1,0:T(8,128)}, u32[]{:S(2)}, u32[]{:S(2)}) async-start(f32[64,2,128,128]{3,2,1,0:T(8,128)} %broadcast_multiply_fusion), calls=%async_computation | async-start | bytes 16777216 | tf_op jit(solution)/shard_map/all_to_all | solution.py:82
  148.1 4.1 collective-permute-start.3
  156.8 128.9 %collective-permute-done.3 = f32[2048]{0:T(1024)S(1)} collective-permute-done((f32[2048]{0:T(1024)S(1)}, f32[2048]{0:T(1024)S(1)}, u32[]{:S(2)}, u32[]{:S(2)}) %collective-permute-start.3) | collective-permute-done | bytes 8224 | tf_op jit(solution)/shard_map/ppermute | solution.py:11
  285.7 5.0 %collective-permute-done.4 = f32[2048]{0:T(1024)S(1)} collective-permute-done((f32[2048]{0:T(1024)S(1)}, f32[2048]{0:T(1024)S(1)}, u32[]{:S(2)}, u32[]{:S(2)}) %collective-permute-start.4) | collective-permute-done | bytes 8224 | tf_op jit(solution)/shard_map/ppermute | solution.py:11
  293.2 37.1 %all-to-all-done = f32[64,2,128,128]{3,2,1,0:T(8,128)} async-done(((f32[64,2,128,128]{3,2,1,0:T(8,128)}), f32[64,2,128,128]{3,2,1,0:T(8,128)}, u32[]{:S(2)}, u32[]{:S(2)}) %all-to-all-start) | async-done | bytes 8388640 | tf_op jit(solution)/shard_map/all_to_all | solution.py:82
  330.3 19.5 %all-to-all-start.2 = ((f32[64,2,128]{2,1,0:T(2,128)}), f32[64,2,128]{2,1,0:T(2,128)S(1)}, u32[]{:S(2)}, u32[]{:S(2)}) async-start(f32[64,2,128]{2,1,0:T(2,128)} %broadcast_multiply_fusion.1), calls=%async_computation.2 | async-start | bytes 131072 | tf_op jit(solution)/shard_map/all_to_all | solution.py:83
  349.8 6.2 %gather_fusion.3 = f32[64,128,128]{2,1,0:T(8,128)} fusion(f32[128,128,128]{2,1,0:T(8,128)} %bitcast.13, s32[1024]{0:T(1024)S(1)} %pad_clamp_fusion), kind=kCustom, calls=%fused_computation.3 | custom fusion | bytes 8388864 | tf_op jit(solution)/shard_map/gather | solution.py:93
  356.0 9.8 %gather_fusion.7 = f32[2048,128]{1,0:T(8,128)} fusion(f32[8192,128]{1,0:T(8,128)} %bitcast.121, s32[2048]{0:T(1024)S(1)} %broadcast_clamp_fusion), kind=kCustom, calls=%fused_computation.7 | custom fusion | bytes 2105344 | tf_op jit(solution)/shard_map/gather | solution.py:116
  365.8 11.0 %all-to-all-start.4 = ((f32[256,1,1,8,128]{4,3,2,1,0:T(8,128)}), f32[256,1,1,8,128]{4,3,2,1,0:T(8,128)S(1)}, u32[]{:S(2)}, u32[]{:S(2)}) async-start(f32[256,1,1,8,128]{4,3,2,1,0:T(8,128)} %bitcast.39), calls=%async_computation.4 | async-start | bytes 2097152 | tf_op jit(solution)/shard_map/all_to_all | solution.py:32
  378.3 29.6 %all-to-all-done.4 = f32[256,1,1,8,128]{4,3,2,1,0:T(8,128)S(1)} async-done(((f32[256,1,1,8,128]{4,3,2,1,0:T(8,128)}), f32[256,1,1,8,128]{4,3,2,1,0:T(8,128)S(1)}, u32[]{:S(2)}, u32[]{:S(2)}) %all-to-all-start.4) | async-done | bytes 1048608 | tf_op jit(solution)/shard_map/all_to_all | solution.py:32
  407.9 11.1 %gather_fusion.8 = f32[1024,128]{1,0:T(8,128)} fusion(f32[4,64,8,128]{3,2,1,0:T(8,128)S(1)} %bitcast.124, s32[1024]{0:T(1024)S(1)} %reshape.420), kind=kCustom, calls=%fused_computation.8 | custom fusion | bytes 1060864 | tf_op jit(solution)/shard_map/gather | solution.py:120
  (91 shorter events, 24.2 us)
Async XLA Ops:
  0.6 14.0 %copy-start = (s32[4,4096]{1,0:T(4,128)S(1)}, s32[4,4096]{1,0:T(4,128)}, u32[]{:S(2)}) copy-start(s32[4,4096]{1,0:T(4,128)} %param.6) | copy-start | bytes 196612
  0.7 3.7 copy-start.1
  4.4 24.9 %copy-start.3 = (s32[256,4]{0,1:T(4,128)S(1)}, s32[256,4]{0,1:T(4,128)}, u32[]{:S(2)}) copy-start(s32[256,4]{0,1:T(4,128)} %param.7) | copy-start | bytes 12292
  6.0 42.5 %collective-permute-start = (f32[2048,128]{1,0:T(8,128)}, f32[2048,128]{1,0:T(8,128)}, u32[]{:S(2)}, u32[]{:S(2)}) collective-permute-start(f32[2048,128]{1,0:T(8,128)} %get-tuple-element.6), channel_id=1, source_target_pairs={{0,64},{64,128},{128,192},{192,0},{1,65},{65,129},{129,193},{193,1... | collective-permute-start | bytes 3145736 | tf_op jit(solution)/shard_map/ppermute | solution.py:11
  14.3 60.7 %collective-permute-start.1 = (f32[2048,128]{1,0:T(8,128)S(1)}, f32[2048,128]{1,0:T(8,128)}, u32[]{:S(2)}, u32[]{:S(2)}) collective-permute-start(f32[2048,128]{1,0:T(8,128)S(1)} %get-tuple-element.8), channel_id=1, source_target_pairs={{0,128},{64,192},{128,0},{192,64},{1,129},{65,193},{129,1},{193,65... | collective-permute-start | bytes 3145736 | tf_op jit(solution)/shard_map/ppermute | solution.py:11
  14.4 62.8 %collective-permute-start.2 = (f32[2048,128]{1,0:T(8,128)S(1)}, f32[2048,128]{1,0:T(8,128)}, u32[]{:S(2)}, u32[]{:S(2)}) collective-permute-start(f32[2048,128]{1,0:T(8,128)S(1)} %get-tuple-element.5), channel_id=1, source_target_pairs={{0,192},{64,0},{128,64},{192,128},{1,193},{65,1},{129,65},{193,129... | collective-permute-start | bytes 3145736 | tf_op jit(solution)/shard_map/ppermute | solution.py:11
  19.5 92.0 %all-to-all-start.1 = ((s32[64,1,2]{2,1,0:T(1,128)}), s32[64,1,2]{2,1,0:T(1,128)S(1)}, u32[]{:S(2)}, u32[]{:S(2)}) async-start(s32[64,1,2]{2,1,0:T(1,128)} %bitcast.14), calls=%async_computation.1 | async-start | bytes 65536 | tf_op jit(solution)/shard_map/all_to_all | solution.py:84
  29.6 12.8 %copy-start.5 = (s32[3]{0:T(128)S(1)}, s32[3]{0:T(128)}, u32[]{:S(2)}) copy-start(s32[3]{0:T(128)} %constant.220) | copy-start | bytes 40
  29.6 12.9 %copy-start.4 = (s32[3]{0:T(128)S(1)}, s32[3]{0:T(128)}, u32[]{:S(2)}) copy-start(s32[3]{0:T(128)} %constant.223) | copy-start | bytes 40
  111.5 30.6 %all-to-all-start.3 = ((s32[256,1,1,8]{3,2,1,0:T(1,128)}), s32[256,1,1,8]{3,2,1,0:T(1,128)S(1)}, u32[]{:S(2)}, u32[]{:S(2)}) async-start(s32[256,1,1,8]{3,2,1,0:T(1,128)} %bitcast.33), calls=%async_computation.3 | async-start | bytes 262144 | tf_op jit(solution)/shard_map/all_to_all | solution.py:32
  136.4 11.7 %copy-start.2 = (f32[4,2048]{1,0:T(4,128)S(1)}, f32[4,2048]{1,0:T(4,128)}, u32[]{:S(2)}) copy-start(f32[4,2048]{1,0:T(4,128)} %param.5) | copy-start | bytes 98308
  142.1 188.2 %all-to-all-start = ((f32[64,2,128,128]{3,2,1,0:T(8,128)}), f32[64,2,128,128]{3,2,1,0:T(8,128)}, u32[]{:S(2)}, u32[]{:S(2)}) async-start(f32[64,2,128,128]{3,2,1,0:T(8,128)} %broadcast_multiply_fusion), calls=%async_computation | async-start | bytes 16777216 | tf_op jit(solution)/shard_map/all_to_all | solution.py:82
  148.1 137.5 %collective-permute-start.3 = (f32[2048]{0:T(1024)S(1)}, f32[2048]{0:T(1024)S(1)}, u32[]{:S(2)}, u32[]{:S(2)}) collective-permute-start(f32[2048]{0:T(1024)S(1)} %bitcast.135), channel_id=1, source_target_pairs={{0,64},{64,128},{128,192},{192,0},{1,65},{65,129},{129,193},{193,1... | collective-permute-start | bytes 24584 | tf_op jit(solution)/shard_map/ppermute | solution.py:11
  152.2 138.5 %collective-permute-start.4 = (f32[2048]{0:T(1024)S(1)}, f32[2048]{0:T(1024)S(1)}, u32[]{:S(2)}, u32[]{:S(2)}) collective-permute-start(f32[2048]{0:T(1024)S(1)} %bitcast.134), channel_id=1, source_target_pairs={{0,128},{64,192},{128,0},{192,64},{1,129},{65,193},{129,1},{193,65... | collective-permute-start | bytes 24584 | tf_op jit(solution)/shard_map/ppermute | solution.py:11
  154.2 137.3 %collective-permute-start.5 = (f32[2048]{0:T(1024)S(1)}, f32[2048]{0:T(1024)S(1)}, u32[]{:S(2)}, u32[]{:S(2)}) collective-permute-start(f32[2048]{0:T(1024)S(1)} %bitcast.133), channel_id=1, source_target_pairs={{0,192},{64,0},{128,64},{192,128},{1,193},{65,1},{129,65},{193,129... | collective-permute-start | bytes 24584 | tf_op jit(solution)/shard_map/ppermute | solution.py:11
  330.3 35.5 %all-to-all-start.2 = ((f32[64,2,128]{2,1,0:T(2,128)}), f32[64,2,128]{2,1,0:T(2,128)S(1)}, u32[]{:S(2)}, u32[]{:S(2)}) async-start(f32[64,2,128]{2,1,0:T(2,128)} %broadcast_multiply_fusion.1), calls=%async_computation.2 | async-start | bytes 131072 | tf_op jit(solution)/shard_map/all_to_all | solution.py:83
  365.8 42.1 %all-to-all-start.4 = ((f32[256,1,1,8,128]{4,3,2,1,0:T(8,128)}), f32[256,1,1,8,128]{4,3,2,1,0:T(8,128)S(1)}, u32[]{:S(2)}, u32[]{:S(2)}) async-start(f32[256,1,1,8,128]{4,3,2,1,0:T(8,128)} %bitcast.39), calls=%async_computation.4 | async-start | bytes 2097152 | tf_op jit(solution)/shard_map/all_to_all | solution.py:32
where the time goes:
time: 420 us; the launch traced here: 419 us
  waiting for transfers between devices  257 us (61%)
  starting transfers between devices  78.8 us (19%)
  local copies, waits for them, and re-layouts  70.3 us (17%)
  other arithmetic  12.2 us (3%)
    ppermute x6, waiting for transfers between devices, shifted(): lax.ppermute(shard, axis, [(i, (i + by) % peers) for i in range(peers)])  159 us
    all_to_all x1, waiting for transfers between devices, body(): lax.all_to_all(send_blocks, 'dev', split_axis=0, concat_axis=0, tiled=True)  37.1 us
    all_to_all x2, waiting for transfers between devices, joined_exchange(): lax.all_to_all(pieces, axis, split_axis=0, concat_axis=0, tiled=True)  35.3 us
    all_to_all x2, starting transfers between devices, joined_exchange(): lax.all_to_all(pieces, axis, split_axis=0, concat_axis=0, tiled=True)  28.7 us
    all_to_all x1, waiting for transfers between devices, body(): lax.all_to_all(send_place, 'dev', split_axis=0, concat_axis=0, tiled=True)  25.4 us
    all_to_all x1, starting transfers between devices, body(): lax.all_to_all(send_sums, 'dev', split_axis=0, concat_axis=0, tiled=True)  19.5 us
    ppermute x6, starting transfers between devices, shifted(): lax.ppermute(shard, axis, [(i, (i + by) % peers) for i in range(peers)])  14.8 us
    gather x1, local copies, waits for them, and re-layouts, body(): looked = returned[table_grid, owner, owner_order]  11.1 us
  transfers between devices with their start and end apart: 11, of which 8 were waited for; matrix products, arithmetic and copies ran while one was open for 16% of the time, Pallas kernels for 0%

commit v1 on v0

v1 whole, which is shorter than its diff:
```python
import jax
import jax.numpy as jnp
from jax import lax
from jax.experimental import pallas as pl
from jax.experimental.pallas import tpu as pltpu
from jax.sharding import PartitionSpec as P

TILE = 128


def spread_rows(tables, parts):
    count, rows, width = tables.shape
    blocks = rows // TILE
    piece = TILE // parts

    def kernel(in_ref, out_ref):
        def one(block, carry):
            for part in range(parts):
                out_ref[part, block] = in_ref[0, pl.ds(block * TILE + part * piece, piece), :]
            return carry

        lax.fori_loop(0, blocks, one, 0)

    return pl.pallas_call(
        kernel,
        grid=(count,),
        in_specs=[pl.BlockSpec((1, rows, width), lambda t: (t, 0, 0))],
        out_specs=pl.BlockSpec((parts, blocks, piece, width), lambda t: (t, 0, 0, 0)),
        out_shape=jax.ShapeDtypeStruct((count * parts, blocks, piece, width), tables.dtype),
        name="spread_rows",
    )(tables)


def place_pieces(pieces, slots, sums, notes, total):
    count, piece, width = pieces.shape
    owners = sums.shape[0]
    per_owner = total // owners
    chunk = 512
    batch = 16

    def kernel(slots_ref, in_ref, sums_ref, notes_ref, out_ref):
        step = pl.program_id(0)

        @pl.when(step == 0)
        def _():
            for owner in range(owners):
                out_ref[owner * per_owner + per_owner - 2] = sums_ref[owner]
                out_ref[owner * per_owner + per_owner - 1] = notes_ref[owner]

        def some(at, carry):
            first = at * batch
            held = [in_ref[first + k] for k in range(batch)]
            for k in range(batch):
                out_ref[slots_ref[step * chunk + first + k]] = held[k]
            return carry

        lax.fori_loop(0, chunk // batch, some, 0)

    return pl.pallas_call(
        kernel,
        grid_spec=pltpu.PrefetchScalarGridSpec(
            num_scalar_prefetch=1,
            grid=(count // chunk,),
            in_specs=[
                pl.BlockSpec((chunk, piece, width), lambda c, s: (c, 0, 0)),
                pl.BlockSpec((owners, piece, width), lambda c, s: (0, 0, 0)),
                pl.BlockSpec((owners, piece, width), lambda c, s: (0, 0, 0)),
            ],
            out_specs=pl.BlockSpec((total, piece, width), lambda c, s: (0, 0, 0)),
        ),
        out_shape=jax.ShapeDtypeStruct((total, piece, width), pieces.dtype),
        name="place_pieces",
    )(slots, pieces, sums, notes)


def pick_rows(rows, which):
    count = which.shape[0]
    width = rows.shape[2]
    batch = 16

    def kernel(which_ref, in_ref, out_ref):
        def some(at, carry):
            first = at * batch
            held = [in_ref[which_ref[first + k]] for k in range(batch)]
            for k in range(batch):
                out_ref[first + k] = held[k]
            return carry

        lax.fori_loop(0, count // batch, some, 0)

    return pl.pallas_call(
        kernel,
        grid_spec=pltpu.PrefetchScalarGridSpec(
            num_scalar_prefetch=1,
            grid=(1,),
            in_specs=[pl.BlockSpec(rows.shape, lambda c, w: (0, 0, 0))],
            out_specs=pl.BlockSpec((count, 1, width), lambda c, w: (0, 0, 0)),
        ),
        out_shape=jax.ShapeDtypeStruct((count, 1, width), rows.dtype),
        name="pick_rows",
    )(which, rows)


def join_rows(got, blocks):
    parts, _, piece, width = got.shape
    chunk = 8

    def kernel(in_ref, out_ref):
        first = pl.program_id(0) * chunk

        def one(block, carry):
            for part in range(parts):
                out_ref[block * parts + part] = in_ref[part, first + block]
            return carry

        lax.fori_loop(0, chunk, one, 0)

    return pl.pallas_call(
        kernel,
        grid=(blocks // chunk,),
        in_specs=[pl.BlockSpec(got.shape, lambda c: (0, 0, 0, 0))],
        out_specs=pl.BlockSpec((chunk * parts, piece, width), lambda c: (c, 0, 0)),
        out_shape=jax.ShapeDtypeStruct((blocks * parts, piece, width), got.dtype),
        name="join_rows",
    )(got)


def swap_groups(parts, axis):
    peers = lax.axis_size(axis)
    me = lax.axis_index(axis)
    held = [lax.dynamic_index_in_dim(parts, me, 0, keepdims=False)]
    for by in range(1, peers):
        part = lax.dynamic_index_in_dim(parts, (me + by) % peers, 0, keepdims=False)
        held.append(lax.ppermute(part, axis, [(i, (i + by) % peers) for i in range(peers)]))
    return jnp.stack(held)[(me - jnp.arange(peers)) % peers]


def body(tables, accum, block_position, lookup_ids):
    groups = lax.axis_size("grp")
    shards = lax.axis_size("dev")
    my_group = lax.axis_index("grp")
    my_shard = lax.axis_index("dev")
    both = ("grp", "dev")
    table_count, old_rows, width = tables.shape
    per_old = old_rows // TILE
    local = groups * per_old
    piece = TILE // shards
    look_rows = lookup_ids.shape[0]
    limit = 2 * look_rows // shards

    spread = spread_rows(tables, shards)
    spread, accum, block_position, lookup_ids = lax.optimization_barrier(
        (spread, accum, block_position, lookup_ids)
    )
    pieces = lax.all_to_all(spread, both, split_axis=0, concat_axis=0, tiled=True)

    table_ids = jnp.arange(table_count, dtype=jnp.int32)[None, :]
    id_place = block_position[table_ids, lookup_ids // TILE]
    owner = id_place // local
    local_row = id_place % local * TILE + lookup_ids % TILE
    owner_marks = (owner[..., None] == jnp.arange(shards, dtype=jnp.int32)[None, None, :]).astype(jnp.int32)
    owner_order = jnp.sum((jnp.cumsum(owner_marks, axis=0) - owner_marks) * owner_marks, axis=2)
    table_grid = jnp.broadcast_to(table_ids, owner.shape)
    asking = (
        jnp.full((table_count, shards, limit), -1, jnp.int32)
        .at[table_grid, owner, owner_order]
        .set(local_row)
    )

    small = jnp.concatenate(
        [
            accum.reshape(table_count, per_old, TILE),
            asking.astype(jnp.float32).reshape(table_count, -1, TILE),
        ],
        axis=1,
    )
    small = swap_groups(small, "grp")
    block_sums = small[:, :per_old].reshape(local, TILE)
    passed = small[:, per_old:].reshape(groups, shards, limit)

    counter = jnp.arange(local, dtype=jnp.int32)
    old_index = (counter // per_old * shards + my_shard) * per_old + counter % per_old
    position_row = lax.dynamic_index_in_dim(block_position, my_group, 0, keepdims=False)
    new_place = position_row[old_index]
    target = new_place // local
    slot_place = new_place % local
    longer = local // 2 + 1
    capacity = -(-longer // shards) + -(-(local - longer) // shards)
    marks = (target[:, None] == jnp.arange(shards, dtype=jnp.int32)[None, :]).astype(jnp.int32)
    order_in = jnp.sum((jnp.cumsum(marks, axis=0) - marks) * marks, axis=1)
    slot_index = target * capacity + order_in
    source_of = jnp.zeros((shards * capacity,), jnp.int32).at[slot_index].set(counter)
    filled = jnp.zeros((shards * capacity,), jnp.int32).at[slot_index].set(1)
    send_sums = block_sums[source_of].reshape(shards, capacity, TILE)
    send_place = jnp.where(filled == 1, slot_place[source_of], -1).reshape(shards, capacity)
    notes = jnp.concatenate(
        [send_place.astype(jnp.float32), passed.transpose(1, 0, 2).reshape(shards, groups * limit)], axis=1
    )
    notes = jnp.pad(notes[:, None, :], ((0, 0), (0, piece - 1), (0, TILE - notes.shape[1])))

    per_owner = local + 2
    slots = position_row + position_row // local * 2
    sending = place_pieces(
        pieces.reshape(-1, piece, width), slots, send_sums, notes, shards * per_owner
    ).reshape(shards, per_owner, piece, width)
    got = lax.all_to_all(sending, "dev", split_axis=0, concat_axis=0, tiled=True)

    got_notes = got[:, local + 1, 0, : capacity + groups * limit].astype(jnp.int32)
    wanted = got_notes[:, capacity:].reshape(shards, groups, limit).transpose(1, 0, 2).reshape(-1)
    wanted = jnp.maximum(wanted, 0)
    inside = wanted % TILE
    at_row = (inside // piece * per_owner + wanted // TILE) * piece + inside % piece
    answer = pick_rows(got.reshape(-1, 1, width), at_row).reshape(groups * shards, limit, width)
    returned = lax.all_to_all(answer, both, split_axis=0, concat_axis=0, tiled=True)

    new_table = join_rows(got, local).reshape(1, local * TILE, width)
    flat_place = got_notes[:, :capacity].reshape(-1)
    landing = jnp.where(flat_place >= 0, flat_place, local)
    picker = (
        jnp.zeros((local,), jnp.int32)
        .at[landing]
        .set(jnp.arange(shards * capacity, dtype=jnp.int32), mode="drop")
    )
    got_sums = got[:, local].reshape(shards * capacity, TILE)
    new_accum = got_sums[picker].reshape(1, local * TILE)

    slot = ((table_grid * shards + owner) * limit + owner_order).reshape(-1)
    looked = pick_rows(returned.reshape(-1, 1, width), slot).reshape(look_rows, table_count, width)
    return (new_table, new_accum, looked)


def solution(mesh):
    placed = (P(None, ("grp", "dev"), None), P(None, ("grp", "dev")), P(), P(("grp", "dev"), None))
    return jax.shard_map(
        body,
        mesh=mesh,
        in_specs=placed,
        out_specs=(P("grp", "dev", None), P("grp", "dev"), P(("grp", "dev"), None, None)),
        check_vma=False,
    )
```

time: 420 us -> 293 us (0.70)
  waiting for transfers between devices: 257 us -> 80.5 us
  blocking collectives: 0 us -> 107 us
  starting transfers between devices: 78.8 us -> 35.6 us
  local copies, waits for them, and re-layouts: 70.3 us -> 29.2 us
  Pallas kernels: 0 us -> 33.2 us
  other arithmetic: 12.2 us -> 5.48 us
    all_to_all x0 -> x1, blocking collectives: none -> 107 us  [body(): lax.all_to_all(sending, 'dev', split_axis=0, concat_axis=0, tiled=True)]
    ppermute x6 -> x3, waiting for transfers between devices: 159 us -> 59.9 us  [swap_groups(): lax.ppermute(part, axis, [(i, (i + by) % peers) for i in range(peers)])]
    all_to_all x5 -> x2, waiting for transfers between devices: 97.8 us -> 20.5 us  [the longest x1 20.5 us: body(): lax.all_to_all(answer, both, split_axis=0, concat_axis=0, tiled=True)]
    all_to_all x5 -> x2, starting transfers between devices: 64 us -> 23.4 us  [the longest x1 16.6 us: body(): lax.all_to_all(spread, both, split_axis=0, concat_axis=0, tiled=True)]
    pallas_call x0 -> x5, Pallas kernels: none -> 33.2 us  [the longest x1 10.9 us: place_pieces(): pl.pallas_call(kernel, grid_spec=pltpu.PrefetchScalarGridSpec(num_scalar_...]
    gather x11 -> x8, local copies, waits for them, and re-layouts: 45 us -> 12.5 us  [the longest x5 9.55 us: body(): id_place = block_position[table_ids, lookup_ids // TILE]]
    mul x2 -> x1, other arithmetic: 7.98 us -> 0.01 us  [body(): slot = ((table_grid * shards + owner) * limit + owner_order).reshape(-1)]
    dynamic_update_slice x7 -> x0, local copies, waits for them, and re-layouts: 7.18 us -> none  [the longest x3 6.79 us: body(): held = lax.dynamic_update_index_in_dim(held, got_rows, anchor, 0)]
  transfers between devices with their start and end apart: 11 -> 5, of which waited for: 8 -> 2; matrix products, arithmetic and copies ran while one was open for 16% -> 10% of each run, Pallas kernels for 0% -> 2%
where the time goes in v1:
time: 293 us; the launch traced here: 292 us
  blocking collectives  107 us (37%)
  waiting for transfers between devices  80.5 us (27%)
  starting transfers between devices  35.6 us (12%)
  Pallas kernels  33.2 us (11%)
  local copies, waits for them, and re-layouts  29.2 us (10%)
  other arithmetic  5.48 us (2%)
    all_to_all x1, blocking collectives, body(): lax.all_to_all(sending, 'dev', split_axis=0, concat_axis=0, tiled=True)  107 us
    ppermute x3, waiting for transfers between devices, swap_groups(): lax.ppermute(part, axis, [(i, (i + by) % peers) for i in range(peers)])  59.9 us
    all_to_all x1, waiting for transfers between devices, body(): lax.all_to_all(answer, both, split_axis=0, concat_axis=0, tiled=True)  20.5 us
    all_to_all x1, starting transfers between devices, body(): lax.all_to_all(spread, both, split_axis=0, concat_axis=0, tiled=True)  16.6 us
    ppermute x3, starting transfers between devices, swap_groups(): lax.ppermute(part, axis, [(i, (i + by) % peers) for i in range(peers)])  12.2 us
    pallas_call x1, Pallas kernels, place_pieces(): pl.pallas_call(kernel, grid_spec=pltpu.PrefetchScalarGridSpec(num_scalar_...  10.9 us
    pallas_call x2, Pallas kernels, pick_rows(): pl.pallas_call(kernel, grid_spec=pltpu.PrefetchScalarGridSpec(num_scalar_...  10 us
    gather x5, local copies, waits for them, and re-layouts, body(): id_place = block_position[table_ids, lookup_ids // TILE]  9.55 us
  transfers between devices with their start and end apart: 5, of which 2 were waited for; matrix products, arithmetic and copies ran while one was open for 10% of the time, Pallas kernels for 2%

profile of v1, /device:TPU:1, one launch (start us, length us, event | category | flops | bytes accessed | tf_op | source)
XLA Modules:
  0.0 292.4 jit_solution(12038913602325254497)
XLA Ops:
  0.6 5.8 %spread_rows.1 = f32[256,16,2,128]{3,2,1,0:T(2,128)} custom-call(f32[4,2048,128]{2,1,0:T(8,128)} %in_ref.1), custom_call_target="tpu_custom_call" | custom-call | tf_op jit(solution)/shard_map/spread_rows/pallas_call | solution.py:24
  6.5 16.6 %all-to-all-start = ((f32[256,16,2,128]{3,2,1,0:T(2,128)}), f32[256,16,2,128]{3,2,1,0:T(2,128)}, u32[]{:S(2)}, u32[]{:S(2)}) async-start(f32[256,16,2,128]{3,2,1,0:T(2,128)} %spread_rows.1), calls=%async_computation | async-start | bytes 8388608 | tf_op jit(solution)/shard_map/all_to_all | solution.py:155
  23.5 9.1 %gather_fusion = s32[1024]{0:T(1024)S(1)} fusion(s32[4,4096]{1,0:T(4,128)S(1)} %copy-done, s32[1024]{0:T(1024)S(1)} %reshape.412), kind=kCustom, calls=%fused_computation | custom fusion | bytes 16384 | tf_op jit(solution)/shard_map/gather | solution.py:158
  33.6 2.4 reduce-window.6
  37.0 4.3 %scatter_custom_fusion.3 = s32[2048]{0:T(1024)S(1)} fusion(s32[1024]{0:T(1024)S(1)} %reshape.482, s32[1024]{0:T(1024)S(1)} %reshape.484, s32[]{:T(128)} %constant.215.clone.1), kind=kCustom, calls=%fused_computation.106 | custom fusion | bytes 8196
  41.7 2.3 collective-permute-start.2
  44.0 4.4 %collective-permute-start.1 = (f32[20,128]{1,0:T(8,128)S(1)}, f32[20,128]{1,0:T(8,128)S(1)}, u32[]{:S(2)}, u32[]{:S(2)}) collective-permute-start(f32[20,128]{1,0:T(8,128)S(1)} %get-tuple-element.13), channel_id=1, source_target_pairs={{0,128},{64,192},{128,0},{192,64},{1,129},{65,193},{129,1},{193,65... | collective-permute-start | bytes 30728 | tf_op jit(solution)/shard_map/ppermute | solution.py:134
  48.4 5.5 %collective-permute-start = (f32[20,128]{1,0:T(8,128)S(1)}, f32[20,128]{1,0:T(8,128)S(1)}, u32[]{:S(2)}, u32[]{:S(2)}) collective-permute-start(f32[20,128]{1,0:T(8,128)S(1)} %get-tuple-element.14), channel_id=1, source_target_pairs={{0,64},{64,128},{128,192},{192,0},{1,65},{65,129},{129,193},{193,1... | collective-permute-start | bytes 30728 | tf_op jit(solution)/shard_map/ppermute | solution.py:134
  54.0 0.8 gather_fusion.2
  56.7 1.2 gather_fusion.4
  58.8 59.9 %collective-permute-done.2 = f32[20,128]{1,0:T(8,128)S(1)} collective-permute-done((f32[20,128]{1,0:T(8,128)S(1)}, f32[20,128]{1,0:T(8,128)S(1)}, u32[]{:S(2)}, u32[]{:S(2)}) %collective-permute-start.2) | collective-permute-done | bytes 10272 | tf_op jit(solution)/shard_map/ppermute | solution.py:134
  119.3 1.2 gather_fusion.3
  121.5 10.9 %place_pieces.1 = f32[4224,2,128]{2,1,0:T(2,128)} custom-call(s32[4096]{0:T(1024)} %fusion.12.slots_ref, f32[4096,2,128]{2,1,0:T(2,128)} %bitcast.1.in_ref, f32[64,2,128]{2,1,0:T(2,128)} %bitcast.123, f32[64,2,128]{2,1,0:T(2,128)} %pad.4.notes_ref), custom_call_target="tpu_custom_call" | custom-call | tf_op jit(solution)/shard_map/place_pieces/pallas_call | solution.py:59
  132.4 107.2 %all_to_all.15.in_ref = f32[64,66,2,128]{3,2,1,0:T(2,128)S(1)} all-to-all(f32[64,66,2,128]{3,2,1,0:T(2,128)} %bitcast.111), channel_id=1, replica_groups=mesh['grp'=4,'dev'=64] {'dev'}, dimensions={0} | all-to-all | bytes 8650752 | tf_op jit(solution)/shard_map/all_to_all | solution.py:206
  239.7 2.0 copy-done.1
  243.4 6.2 %pick_rows.2 = f32[2048,1,128]{2,1,0:T(1,128)} custom-call(s32[2048]{0:T(1024)} %fusion.17.which_ref, f32[8448,1,128]{2,1,0:T(1,128)} %bitcast.108), custom_call_target="tpu_custom_call" | custom-call | tf_op jit(solution)/shard_map/pick_rows/pallas_call | solution.py:91
  249.6 6.8 %all-to-all-start.2 = ((f32[256,8,128]{2,1,0:T(8,128)}), f32[256,8,128]{2,1,0:T(8,128)S(1)}, u32[]{:S(2)}, u32[]{:S(2)}) async-start(f32[256,8,128]{2,1,0:T(8,128)} %bitcast.115), calls=%async_computation.2 | async-start | bytes 2097152 | tf_op jit(solution)/shard_map/all_to_all | solution.py:214
  257.6 1.0 scatter_custom_fusion.2
  258.5 0.8 slice.48
  259.4 1.2 gather_fusion.5
  260.6 6.5 %join_rows.1 = f32[4096,2,128]{2,1,0:T(2,128)} custom-call(f32[64,66,2,128]{3,2,1,0:T(2,128)} %copy-done.1), custom_call_target="tpu_custom_call" | custom-call | tf_op jit(solution)/shard_map/join_rows/pallas_call | solution.py:118
  267.1 20.5 %all-to-all-done.2 = f32[256,8,128]{2,1,0:T(8,128)S(1)} async-done(((f32[256,8,128]{2,1,0:T(8,128)}), f32[256,8,128]{2,1,0:T(8,128)S(1)}, u32[]{:S(2)}, u32[]{:S(2)}) %all-to-all-start.2) | async-done | bytes 1048608 | tf_op jit(solution)/shard_map/all_to_all | solution.py:214
  287.6 1.0 copy-done.2
  288.6 3.8 %pick_rows.3 = f32[1024,1,128]{2,1,0:T(1,128)} custom-call(s32[1024]{0:T(1024)} %fusion.28.which_ref, f32[2048,1,128]{2,1,0:T(1,128)} %bitcast.114), custom_call_target="tpu_custom_call" | custom-call | tf_op jit(solution)/shard_map/pick_rows/pallas_call | solution.py:91
  (98 shorter events, 9.6 us)
Async XLA Ops:
  0.6 22.8 %copy-start = (s32[4,4096]{1,0:T(4,128)S(1)}, s32[4,4096]{1,0:T(4,128)}, u32[]{:S(2)}) copy-start(s32[4,4096]{1,0:T(4,128)} %param.6) | copy-start | bytes 196612
  6.5 16.7 %copy-start.4 = (s32[256,4]{0,1:T(4,128)S(1)}, s32[256,4]{0,1:T(4,128)}, u32[]{:S(2)}) copy-start(s32[256,4]{0,1:T(4,128)} %param.7) | copy-start | bytes 12292
  6.5 115.1 %all-to-all-start = ((f32[256,16,2,128]{3,2,1,0:T(2,128)}), f32[256,16,2,128]{3,2,1,0:T(2,128)}, u32[]{:S(2)}, u32[]{:S(2)}) async-start(f32[256,16,2,128]{3,2,1,0:T(2,128)} %spread_rows.1), calls=%async_computation | async-start | bytes 8388608 | tf_op jit(solution)/shard_map/all_to_all | solution.py:155
  23.5 13.1 %copy-start.6 = (s32[3]{0:T(128)S(1)}, s32[3]{0:T(128)}, u32[]{:S(2)}) copy-start(s32[3]{0:T(128)} %constant.231) | copy-start | bytes 40
  23.5 13.1 %copy-start.5 = (s32[3]{0:T(128)S(1)}, s32[3]{0:T(128)}, u32[]{:S(2)}) copy-start(s32[3]{0:T(128)} %constant.234) | copy-start | bytes 40
  23.5 18.1 %copy-start.3 = (f32[4,2048]{1,0:T(4,128)S(1)}, f32[4,2048]{1,0:T(4,128)}, u32[]{:S(2)}) copy-start(f32[4,2048]{1,0:T(4,128)} %param.5) | copy-start | bytes 98308
  41.7 77.0 %collective-permute-start.2 = (f32[20,128]{1,0:T(8,128)S(1)}, f32[20,128]{1,0:T(8,128)S(1)}, u32[]{:S(2)}, u32[]{:S(2)}) collective-permute-start(f32[20,128]{1,0:T(8,128)S(1)} %get-tuple-element.12), channel_id=1, source_target_pairs={{0,192},{64,0},{128,64},{192,128},{1,193},{65,1},{129,65},{193,129... | collective-permute-start | bytes 30728 | tf_op jit(solution)/shard_map/ppermute | solution.py:134
  44.0 74.7 %collective-permute-start.1 = (f32[20,128]{1,0:T(8,128)S(1)}, f32[20,128]{1,0:T(8,128)S(1)}, u32[]{:S(2)}, u32[]{:S(2)}) collective-permute-start(f32[20,128]{1,0:T(8,128)S(1)} %get-tuple-element.13), channel_id=1, source_target_pairs={{0,128},{64,192},{128,0},{192,64},{1,129},{65,193},{129,1},{193,65... | collective-permute-start | bytes 30728 | tf_op jit(solution)/shard_map/ppermute | solution.py:134
  48.4 70.3 %collective-permute-start = (f32[20,128]{1,0:T(8,128)S(1)}, f32[20,128]{1,0:T(8,128)S(1)}, u32[]{:S(2)}, u32[]{:S(2)}) collective-permute-start(f32[20,128]{1,0:T(8,128)S(1)} %get-tuple-element.14), channel_id=1, source_target_pairs={{0,64},{64,128},{128,192},{192,0},{1,65},{65,129},{129,193},{193,1... | collective-permute-start | bytes 30728 | tf_op jit(solution)/shard_map/ppermute | solution.py:134
  239.7 2.0 copy-start.1
  249.6 38.0 %all-to-all-start.2 = ((f32[256,8,128]{2,1,0:T(8,128)}), f32[256,8,128]{2,1,0:T(8,128)S(1)}, u32[]{:S(2)}, u32[]{:S(2)}) async-start(f32[256,8,128]{2,1,0:T(8,128)} %bitcast.115), calls=%async_computation.2 | async-start | bytes 2097152 | tf_op jit(solution)/shard_map/all_to_all | solution.py:214
  287.6 1.0 copy-start.2

commit v2 on v1

v2 whole, which is shorter than its diff:
```python
import jax
import jax.numpy as jnp
from jax import lax
from jax.experimental import pallas as pl
from jax.experimental.pallas import tpu as pltpu
from jax.sharding import PartitionSpec as P

TILE = 128


VMEM = pl.BlockSpec(memory_space=pltpu.VMEM)
SMEM = pl.BlockSpec(memory_space=pltpu.SMEM)
HBM = pl.BlockSpec(memory_space=pltpu.HBM)
ROOM = pltpu.CompilerParams(vmem_limit_bytes=16 * 2**20)


def spread_rows(tables, parts):
    count, rows, width = tables.shape
    blocks = rows // TILE
    piece = TILE // parts
    shape = (count * parts, blocks, piece, width)

    def kernel(in_ref, out_ref, held, came, left):
        def fetch(table):
            return pltpu.make_async_copy(in_ref.at[table], held.at[table], came.at[table])

        def table_out(table):
            return out_ref.at[pl.ds(table * parts, parts)]

        for table in range(count):
            fetch(table).start()
        for table in range(count):
            fetch(table).wait()
            for block in range(blocks):
                pltpu.make_async_copy(held.at[table, block], table_out(table).at[:, block], left.at[table]).start()
        for table in range(count):
            pltpu.make_async_copy(table_out(table), table_out(table), left.at[table]).wait()

    return pl.pallas_call(
        kernel,
        in_specs=[HBM],
        out_specs=HBM,
        out_shape=jax.ShapeDtypeStruct(shape, tables.dtype),
        scratch_shapes=[
            pltpu.VMEM((count, blocks, parts, piece, width), tables.dtype),
            pltpu.SemaphoreType.DMA((count,)),
            pltpu.SemaphoreType.DMA((count,)),
        ],
        name="spread_rows",
    )(tables.reshape(count, blocks, parts, piece, width))


def place_pieces(pieces, slots, sums, notes, total):
    count, piece, width = pieces.shape
    owners = sums.shape[0]
    per_owner = total // owners
    chunk = 512
    steps = count // chunk
    batch = 64

    def kernel(slots_ref, in_ref, sums_ref, notes_ref, out_ref, held, places, came, told):
        def fetch(step):
            span = pl.ds(step * chunk, chunk)
            return pltpu.make_async_copy(in_ref.at[span], held.at[span], came.at[step])

        listing = pltpu.make_async_copy(slots_ref, places, told)
        listing.start()
        for step in range(steps):
            fetch(step).start()
        for owner in range(owners):
            out_ref[owner * per_owner + per_owner - 2] = sums_ref[owner]
            out_ref[owner * per_owner + per_owner - 1] = notes_ref[owner]
        listing.wait()

        def one(step, carry):
            fetch(step).wait()

            def some(at, carry):
                first = step * chunk + at * batch
                rows = [held[first + k] for k in range(batch)]
                for k in range(batch):
                    out_ref[places[first + k]] = rows[k]
                return carry

            return lax.fori_loop(0, chunk // batch, some, carry)

        lax.fori_loop(0, steps, one, 0)

    return pl.pallas_call(
        kernel,
        in_specs=[HBM, HBM, VMEM, VMEM],
        out_specs=VMEM,
        out_shape=jax.ShapeDtypeStruct((total, piece, width), pieces.dtype),
        scratch_shapes=[
            pltpu.VMEM((count, piece, width), pieces.dtype),
            pltpu.SMEM((count,), jnp.int32),
            pltpu.SemaphoreType.DMA((steps,)),
            pltpu.SemaphoreType.DMA,
        ],
        compiler_params=ROOM,
        name="place_pieces",
    )(slots, pieces, sums, notes)


def pick_loop(which_ref, in_ref, out_ref, spots, stride):
    batch = 32

    def one(line, carry):
        for first in range(0, len(spots), batch):
            rows = [in_ref[which_ref[line, k]] for k in range(first, first + batch)]
            for k in range(batch):
                out_ref[line * stride + spots[first + k]] = rows[k]
        return carry

    lax.fori_loop(0, which_ref.shape[0], one, 0)


def pick_rows(rows, which):
    lines, lanes = which.shape
    width = rows.shape[2]

    def kernel(which_ref, in_ref, out_ref):
        pick_loop(which_ref, in_ref, out_ref, range(lanes), lanes)

    return pl.pallas_call(
        kernel,
        in_specs=[SMEM, VMEM],
        out_specs=VMEM,
        out_shape=jax.ShapeDtypeStruct((lines * lanes, 1, width), rows.dtype),
        compiler_params=ROOM,
        name="pick_rows",
    )(which, rows)


def answer_and_join(got, which, blocks, spots, stride):
    parts, _, piece, width = got.shape

    def kernel(which_ref, rows_ref, got_ref, out_ref, table_ref, sums_ref, left):
        for part in range(parts):
            pltpu.make_async_copy(got_ref.at[part, pl.ds(0, blocks)], table_ref.at[:, part], left).start()
        for part in range(parts):
            sums_ref[part] = got_ref[part, blocks]
        pick_loop(which_ref, rows_ref, out_ref, spots, stride)
        pltpu.make_async_copy(table_ref, table_ref, left).wait()

    return pl.pallas_call(
        kernel,
        in_specs=[SMEM, VMEM, VMEM],
        out_specs=(VMEM, HBM, VMEM),
        out_shape=(
            jax.ShapeDtypeStruct((parts * len(spots), 1, width), got.dtype),
            jax.ShapeDtypeStruct((blocks, parts, piece, width), got.dtype),
            jax.ShapeDtypeStruct((parts, piece, width), got.dtype),
        ),
        scratch_shapes=[pltpu.SemaphoreType.DMA],
        compiler_params=ROOM,
        name="answer_and_join",
    )(which, got.reshape(-1, 1, width), got)


def swap_groups(parts, axis):
    peers = lax.axis_size(axis)
    me = lax.axis_index(axis)
    held = [lax.dynamic_index_in_dim(parts, me, 0, keepdims=False)]
    for by in range(1, peers):
        part = lax.dynamic_index_in_dim(parts, (me + by) % peers, 0, keepdims=False)
        held.append(lax.ppermute(part, axis, [(i, (i + by) % peers) for i in range(peers)]))
    return jnp.stack(held)[(me - jnp.arange(peers)) % peers]


def body(tables, accum, block_position, lookup_ids):
    groups = lax.axis_size("grp")
    shards = lax.axis_size("dev")
    my_group = lax.axis_index("grp")
    my_shard = lax.axis_index("dev")
    both = ("grp", "dev")
    table_count, old_rows, width = tables.shape
    per_old = old_rows // TILE
    local = groups * per_old
    piece = TILE // shards
    look_rows = lookup_ids.shape[0]
    limit = 2 * look_rows // shards

    spread = spread_rows(tables, shards)
    spread, accum, block_position, lookup_ids = lax.optimization_barrier(
        (spread, accum, block_position, lookup_ids)
    )
    pieces = lax.all_to_all(spread, both, split_axis=0, concat_axis=0, tiled=True)

    table_ids = jnp.arange(table_count, dtype=jnp.int32)[None, :]
    id_place = block_position[table_ids, lookup_ids // TILE]
    owner = id_place // local
    per_owner = local + 2
    inside = lookup_ids % TILE
    at_row = (inside // piece * per_owner + id_place % local) * piece + inside % piece
    owner_marks = (owner[..., None] == jnp.arange(shards, dtype=jnp.int32)[None, None, :]).astype(jnp.int32)
    owner_order = jnp.sum((jnp.cumsum(owner_marks, axis=0) - owner_marks) * owner_marks, axis=2)
    table_grid = jnp.broadcast_to(table_ids, owner.shape)
    asking = (
        jnp.zeros((table_count, shards, limit), jnp.int32)
        .at[table_grid, owner, owner_order]
        .set(at_row)
    )

    slot = ((table_grid * shards + owner) * limit + owner_order).reshape(-1, TILE)

    small = jnp.concatenate(
        [
            accum.reshape(table_count, per_old, TILE),
            asking.astype(jnp.float32).reshape(table_count, -1, TILE),
        ],
        axis=1,
    )
    small = swap_groups(small, "grp")
    block_sums = small[:, :per_old].reshape(local, TILE)
    passed = small[:, per_old:].reshape(groups, shards, limit)

    counter = jnp.arange(local, dtype=jnp.int32)
    old_index = (counter // per_old * shards + my_shard) * per_old + counter % per_old
    position_row = lax.dynamic_index_in_dim(block_position, my_group, 0, keepdims=False)
    new_place = position_row[old_index]
    target = new_place // local
    slot_place = new_place % local
    longer = local // 2 + 1
    capacity = -(-longer // shards) + -(-(local - longer) // shards)
    marks = (target[:, None] == jnp.arange(shards, dtype=jnp.int32)[None, :]).astype(jnp.int32)
    order_in = jnp.sum((jnp.cumsum(marks, axis=0) - marks) * marks, axis=1)
    slot_index = target * capacity + order_in
    source_of = jnp.zeros((shards * capacity,), jnp.int32).at[slot_index].set(counter)
    filled = jnp.zeros((shards * capacity,), jnp.int32).at[slot_index].set(1)
    send_sums = block_sums[source_of].reshape(shards, capacity, TILE)
    send_place = jnp.where(filled == 1, slot_place[source_of], -1).reshape(shards, capacity)
    notes = jnp.concatenate(
        [passed.transpose(1, 0, 2).reshape(shards, groups * limit), send_place.astype(jnp.float32)], axis=1
    )
    notes = jnp.pad(notes[:, None, :], ((0, 0), (0, piece - 1), (0, TILE - notes.shape[1])))

    pieces, slot = lax.optimization_barrier((pieces, slot))

    slots = position_row + position_row // local * 2
    sending = place_pieces(
        pieces.reshape(-1, piece, width), slots, send_sums, notes, shards * per_owner
    ).reshape(shards, per_owner, piece, width)
    got = lax.all_to_all(sending, "dev", split_axis=0, concat_axis=0, tiled=True)

    asked = groups * limit
    got_notes = got[:, local + 1, 0].astype(jnp.int32)
    spots = [(k // limit * shards) * limit + k % limit for k in range(asked)]
    answer, new_table, got_sums = answer_and_join(got, got_notes, local, spots, limit)
    answer = answer.reshape(groups * shards, limit, width)
    returned = lax.all_to_all(answer, both, split_axis=0, concat_axis=0, tiled=True)

    new_table = new_table.reshape(1, local * TILE, width)
    got_sums, late_notes = lax.optimization_barrier((got_sums, got_notes))
    flat_place = late_notes[:, asked : asked + capacity].reshape(-1)
    landing = jnp.where(flat_place >= 0, flat_place, local)
    picker = (
        jnp.zeros((local,), jnp.int32)
        .at[landing]
        .set(jnp.arange(shards * capacity, dtype=jnp.int32), mode="drop")
    )
    new_accum = got_sums.reshape(shards * capacity, TILE)[picker].reshape(1, local * TILE)

    looked = pick_rows(returned.reshape(-1, 1, width), slot)
    looked = looked.reshape(look_rows, table_count, width)
    return (new_table, new_accum, looked)


def solution(mesh):
    placed = (P(None, ("grp", "dev"), None), P(None, ("grp", "dev")), P(), P(("grp", "dev"), None))
    return jax.shard_map(
        body,
        mesh=mesh,
        in_specs=placed,
        out_specs=(P("grp", "dev", None), P("grp", "dev"), P(("grp", "dev"), None, None)),
        check_vma=False,
    )
```

time: 293 us -> 276 us (0.942)
  Pallas kernels: 33.2 us -> 15.4 us
  waiting for transfers between devices: 80.5 us -> 93.7 us
  local copies, waits for them, and re-layouts: 29.2 us -> 23.3 us
  starting transfers between devices: 35.6 us -> 30.7 us
    pallas_call x5 -> x4, Pallas kernels: 33.2 us -> 15.4 us  [the longest x1 5.77 us: place_pieces(): pl.pallas_call(kernel, in_specs=[HBM, HBM, VMEM, VMEM], out_specs=VMEM, o...]
    all_to_all x1, waiting for transfers between devices: 20.5 us -> 28.8 us  [body(): lax.all_to_all(answer, both, split_axis=0, concat_axis=0, tiled=True)]
    ppermute x3, waiting for transfers between devices: 59.9 us -> 64.9 us  [swap_groups(): lax.ppermute(part, axis, [(i, (i + by) % peers) for i in range(peers)])]
    ppermute x3, starting transfers between devices: 12.2 us -> 7.56 us  [swap_groups(): lax.ppermute(part, axis, [(i, (i + by) % peers) for i in range(peers)])]
    unnamed x18 -> x14, local copies, waits for them, and re-layouts: 7.58 us -> 4.61 us
  transfers between devices with their start and end apart: 5 -> 5, of which waited for: 2 -> 4; matrix products, arithmetic and copies ran while one was open for 10% -> 10% of each run, Pallas kernels for 2% -> 0%
where the time goes in v2:
time: 276 us; the launch traced here: 275 us
  blocking collectives  107 us (39%)
  waiting for transfers between devices  93.7 us (34%)
  starting transfers between devices  30.7 us (11%)
  local copies, waits for them, and re-layouts  23.3 us (8%)
  Pallas kernels  15.4 us (6%)
  other arithmetic  3.5 us (1%)
    all_to_all x1, blocking collectives, body(): lax.all_to_all(sending, 'dev', split_axis=0, concat_axis=0, tiled=True)  107 us
    ppermute x3, waiting for transfers between devices, swap_groups(): lax.ppermute(part, axis, [(i, (i + by) % peers) for i in range(peers)])  64.9 us
    all_to_all x1, waiting for transfers between devices, body(): lax.all_to_all(answer, both, split_axis=0, concat_axis=0, tiled=True)  28.8 us
    all_to_all x1, starting transfers between devices, body(): lax.all_to_all(spread, both, split_axis=0, concat_axis=0, tiled=True)  16.7 us
    gather x5, local copies, waits for them, and re-layouts, body(): id_place = block_position[table_ids, lookup_ids // TILE]  9.54 us
    ppermute x3, starting transfers between devices, swap_groups(): lax.ppermute(part, axis, [(i, (i + by) % peers) for i in range(peers)])  7.56 us
    all_to_all x1, starting transfers between devices, body(): lax.all_to_all(answer, both, split_axis=0, concat_axis=0, tiled=True)  6.51 us
    pallas_call x1, Pallas kernels, place_pieces(): pl.pallas_call(kernel, in_specs=[HBM, HBM, VMEM, VMEM], out_specs=VMEM, o...  5.77 us
  transfers between devices with their start and end apart: 5, of which 4 were waited for; matrix products, arithmetic and copies ran while one was open for 10% of the time, Pallas kernels for 0%

profile of v2, /device:TPU:1, one launch (start us, length us, event | category | flops | bytes accessed | tf_op | source)
XLA Modules:
  0.0 275.3 jit_solution(15469421362270271041)
XLA Ops:
  0.6 3.3 %spread_rows.1 = f32[256,16,2,128]{3,2,1,0:T(2,128)} custom-call(f32[4,16,64,2,128]{4,3,2,1,0:T(2,128)} %bitcast.123), custom_call_target="tpu_custom_call" | custom-call | tf_op jit(solution)/shard_map/spread_rows/pallas_call | solution.py:39
  3.9 16.7 %all-to-all-start = ((f32[256,16,2,128]{3,2,1,0:T(2,128)}), f32[256,16,2,128]{3,2,1,0:T(2,128)}, u32[]{:S(2)}, u32[]{:S(2)}) async-start(f32[256,16,2,128]{3,2,1,0:T(2,128)} %spread_rows.1), calls=%async_computation | async-start | bytes 8388608 | tf_op jit(solution)/shard_map/all_to_all | solution.py:188
  20.9 9.1 %gather_fusion = s32[1024]{0:T(1024)S(1)} fusion(s32[4,4096]{1,0:T(4,128)S(1)} %copy-done, s32[1024]{0:T(1024)S(1)} %reshape.400), kind=kCustom, calls=%fused_computation | custom fusion | bytes 16384 | tf_op jit(solution)/shard_map/gather | solution.py:191
  30.7 2.4 reduce-window.6
  34.5 4.3 %scatter_custom_fusion.3 = s32[2048]{0:T(1024)S(1)} fusion(s32[1024]{0:T(1024)S(1)} %reshape.470, s32[1024]{0:T(1024)S(1)} %reshape.472, s32[]{:T(128)} %constant.188.clone.1), kind=kCustom, calls=%fused_computation.96 | custom fusion | bytes 8196
  39.2 6.5 %collective-permute-start = (f32[20,128]{1,0:T(8,128)S(1)}, f32[20,128]{1,0:T(8,128)S(1)}, u32[]{:S(2)}, u32[]{:S(2)}) collective-permute-start(f32[20,128]{1,0:T(8,128)S(1)} %get-tuple-element.28), channel_id=1, source_target_pairs={{0,64},{64,128},{128,192},{192,0},{1,65},{65,129},{129,193},{193,1... | collective-permute-start | bytes 30728 | tf_op jit(solution)/shard_map/ppermute | solution.py:167
  45.7 1.0 collective-permute-start.1
  46.9 0.8 gather_fusion.2
  48.1 0.8 scatter_custom_fusion
  48.9 0.8 scatter_custom_fusion.1
  49.9 1.2 gather_fusion.4
  51.4 48.9 %collective-permute-done = f32[20,128]{1,0:T(8,128)S(1)} collective-permute-done((f32[20,128]{1,0:T(8,128)S(1)}, f32[20,128]{1,0:T(8,128)S(1)}, u32[]{:S(2)}, u32[]{:S(2)}) %collective-permute-start) | collective-permute-done | bytes 10272 | tf_op jit(solution)/shard_map/ppermute | solution.py:167
  100.3 15.6 %collective-permute-done.1 = f32[20,128]{1,0:T(8,128)S(1)} collective-permute-done((f32[20,128]{1,0:T(8,128)S(1)}, f32[20,128]{1,0:T(8,128)S(1)}, u32[]{:S(2)}, u32[]{:S(2)}) %collective-permute-start.1) | collective-permute-done | bytes 10272 | tf_op jit(solution)/shard_map/ppermute | solution.py:167
  115.9 0.4 collective-permute-done.2
  116.3 0.6 gather_fusion.1
  117.1 0.7 gather_fusion.3
  117.9 5.8 %place_pieces.1 = f32[4224,2,128]{2,1,0:T(2,128)S(1)} custom-call(s32[4096]{0:T(1024)S(1)} %fusion.10.slots_ref, f32[4096,2,128]{2,1,0:T(2,128)} %bitcast.7.in_ref, f32[64,2,128]{2,1,0:T(2,128)S(1)} %bitcast.119, f32[64,2,128]{2,1,0:T(2,128)S(1)} %pad.4.notes_ref), custom_call_target="tpu_custom_call" | custom-call | tf_op jit(solution)/shard_map/place_pieces/pallas_call | solution.py:89
  123.7 107.5 %all_to_all.15.got_ref = f32[64,66,2,128]{3,2,1,0:T(2,128)S(1)} all-to-all(f32[64,66,2,128]{3,2,1,0:T(2,128)S(1)} %bitcast.114), channel_id=1, replica_groups=mesh['grp'=4,'dev'=64] {'dev'}, dimensions={0} | all-to-all | bytes 8650752 | tf_op jit(solution)/shard_map/all_to_all | solution.py:244
  231.2 4.1 %answer_and_join.1 = (f32[2048,1,128]{2,1,0:T(1,128)}, f32[64,64,2,128]{3,2,1,0:T(2,128)}, f32[64,2,128]{2,1,0:T(2,128)S(1)}) custom-call(s32[64,128]{1,0:T(8,128)S(1)} %bitcast.117, f32[8448,1,128]{2,1,0:T(1,128)S(1)} %bitcast.113, f32[64,66,2,128]{3,2,1,0:T(2,128)S(1)} %all_to_all.15.got_ref), custom_call_target="tpu_custom_call" | custom-call | tf_op jit(solution)/shard_map/answer_and_join/pallas_call | solution.py:146
  235.3 6.5 %all-to-all-start.2 = ((f32[256,8,128]{2,1,0:T(8,128)}), f32[256,8,128]{2,1,0:T(8,128)S(1)}, u32[]{:S(2)}, u32[]{:S(2)}) async-start(f32[256,8,128]{2,1,0:T(8,128)} %bitcast.34), calls=%async_computation.2 | async-start | bytes 2097152 | tf_op jit(solution)/shard_map/all_to_all | solution.py:251
  242.1 1.0 scatter_custom_fusion.2
  243.1 1.2 gather_fusion.5
  244.3 28.8 %all-to-all-done.2 = f32[256,8,128]{2,1,0:T(8,128)S(1)} async-done(((f32[256,8,128]{2,1,0:T(8,128)}), f32[256,8,128]{2,1,0:T(8,128)S(1)}, u32[]{:S(2)}, u32[]{:S(2)}) %all-to-all-start.2) | async-done | bytes 1048608 | tf_op jit(solution)/shard_map/all_to_all | solution.py:251
  273.0 2.2 pick_rows.1
  (81 shorter events, 4.1 us)
Async XLA Ops:
  0.6 20.3 %copy-start = (s32[4,4096]{1,0:T(4,128)S(1)}, s32[4,4096]{1,0:T(4,128)}, u32[]{:S(2)}) copy-start(s32[4,4096]{1,0:T(4,128)} %param.6) | copy-start | bytes 196612
  3.9 16.7 %copy-start.2 = (s32[256,4]{0,1:T(4,128)S(1)}, s32[256,4]{0,1:T(4,128)}, u32[]{:S(2)}) copy-start(s32[256,4]{0,1:T(4,128)} %param.7) | copy-start | bytes 12292
  3.9 114.0 %all-to-all-start = ((f32[256,16,2,128]{3,2,1,0:T(2,128)}), f32[256,16,2,128]{3,2,1,0:T(2,128)}, u32[]{:S(2)}, u32[]{:S(2)}) async-start(f32[256,16,2,128]{3,2,1,0:T(2,128)} %spread_rows.1), calls=%async_computation | async-start | bytes 8388608 | tf_op jit(solution)/shard_map/all_to_all | solution.py:188
  20.9 12.8 %copy-start.4 = (s32[3]{0:T(128)S(1)}, s32[3]{0:T(128)}, u32[]{:S(2)}) copy-start(s32[3]{0:T(128)} %constant.209) | copy-start | bytes 40
  20.9 12.9 %copy-start.3 = (s32[3]{0:T(128)S(1)}, s32[3]{0:T(128)}, u32[]{:S(2)}) copy-start(s32[3]{0:T(128)} %constant.212) | copy-start | bytes 40
  20.9 18.2 %copy-start.1 = (f32[4,2048]{1,0:T(4,128)S(1)}, f32[4,2048]{1,0:T(4,128)}, u32[]{:S(2)}) copy-start(f32[4,2048]{1,0:T(4,128)} %param.5) | copy-start | bytes 98308
  39.2 61.2 %collective-permute-start = (f32[20,128]{1,0:T(8,128)S(1)}, f32[20,128]{1,0:T(8,128)S(1)}, u32[]{:S(2)}, u32[]{:S(2)}) collective-permute-start(f32[20,128]{1,0:T(8,128)S(1)} %get-tuple-element.28), channel_id=1, source_target_pairs={{0,64},{64,128},{128,192},{192,0},{1,65},{65,129},{129,193},{193,1... | collective-permute-start | bytes 30728 | tf_op jit(solution)/shard_map/ppermute | solution.py:167
  45.7 70.2 %collective-permute-start.1 = (f32[20,128]{1,0:T(8,128)S(1)}, f32[20,128]{1,0:T(8,128)S(1)}, u32[]{:S(2)}, u32[]{:S(2)}) collective-permute-start(f32[20,128]{1,0:T(8,128)S(1)} %get-tuple-element.27), channel_id=1, source_target_pairs={{0,128},{64,192},{128,0},{192,64},{1,129},{65,193},{129,1},{193,65... | collective-permute-start | bytes 30728 | tf_op jit(solution)/shard_map/ppermute | solution.py:167
  46.7 69.6 %collective-permute-start.2 = (f32[20,128]{1,0:T(8,128)S(1)}, f32[20,128]{1,0:T(8,128)S(1)}, u32[]{:S(2)}, u32[]{:S(2)}) collective-permute-start(f32[20,128]{1,0:T(8,128)S(1)} %get-tuple-element.26), channel_id=1, source_target_pairs={{0,192},{64,0},{128,64},{192,128},{1,193},{65,1},{129,65},{193,129... | collective-permute-start | bytes 30728 | tf_op jit(solution)/shard_map/ppermute | solution.py:167
  235.3 37.7 %all-to-all-start.2 = ((f32[256,8,128]{2,1,0:T(8,128)}), f32[256,8,128]{2,1,0:T(8,128)S(1)}, u32[]{:S(2)}, u32[]{:S(2)}) async-start(f32[256,8,128]{2,1,0:T(8,128)} %bitcast.34), calls=%async_computation.2 | async-start | bytes 2097152 | tf_op jit(solution)/shard_map/all_to_all | solution.py:251

commit v3 on v2

--- a/solution.py
+++ b/solution.py
@@ -18,14 +18,14 @@
     count, rows, width = tables.shape
     blocks = rows // TILE
     piece = TILE // parts
-    shape = (count * parts, blocks, piece, width)
+    shape = (parts, count, blocks, piece, width)
 
     def kernel(in_ref, out_ref, held, came, left):
         def fetch(table):
             return pltpu.make_async_copy(in_ref.at[table], held.at[table], came.at[table])
 
         def table_out(table):
-            return out_ref.at[pl.ds(table * parts, parts)]
+            return out_ref.at[:, table]
 
         for table in range(count):
             fetch(table).start()
@@ -50,27 +50,38 @@
     )(tables.reshape(count, blocks, parts, piece, width))
 
 
-def place_pieces(pieces, slots, sums, notes, total):
+def place_pieces(pieces, listing, smalls, owners, total):
     count, piece, width = pieces.shape
-    owners = sums.shape[0]
     per_owner = total // owners
     chunk = 512
     steps = count // chunk
     batch = 64
-
-    def kernel(slots_ref, in_ref, sums_ref, notes_ref, out_ref, held, places, came, told):
+    lines = smalls[0].shape[0] - owners
+
+    def kernel(list_ref, in_ref, *refs):
+        small_refs = refs[: len(smalls)]
+        out_ref, held, places, sums, notes, came, told = refs[len(smalls) :]
+
         def fetch(step):
             span = pl.ds(step * chunk, chunk)
             return pltpu.make_async_copy(in_ref.at[span], held.at[span], came.at[step])
 
-        listing = pltpu.make_async_copy(slots_ref, places, told)
-        listing.start()
+        telling = pltpu.make_async_copy(list_ref, places, told)
+        telling.start()
         for step in range(steps):
             fetch(step).start()
+        for at, small_ref in enumerate(small_refs):
+            for line in range(lines):
+                sums[at * lines + line] = small_ref[line : line + 1]
+        notes[...] = sum(small_ref[lines:] for small_ref in small_refs)
         for owner in range(owners):
-            out_ref[owner * per_owner + per_owner - 2] = sums_ref[owner]
-            out_ref[owner * per_owner + per_owner - 1] = notes_ref[owner]
-        listing.wait()
+            out_ref[owner * per_owner + per_owner - 1, 0:1] = notes[owner : owner + 1]
+            out_ref[owner * per_owner + per_owner - 1, 1:2] = jnp.zeros((1, width), pieces.dtype)
+        telling.wait()
+        for owner in range(owners):
+            for at in range(piece):
+                row = sums[places[count + owner * piece + at]]
+                out_ref[owner * per_owner + per_owner - 2, at : at + 1] = row
 
         def one(step, carry):
             fetch(step).wait()
@@ -88,28 +99,31 @@
 
     return pl.pallas_call(
         kernel,
-        in_specs=[HBM, HBM, VMEM, VMEM],
+        in_specs=[HBM, HBM] + [VMEM] * len(smalls),
         out_specs=VMEM,
         out_shape=jax.ShapeDtypeStruct((total, piece, width), pieces.dtype),
         scratch_shapes=[
             pltpu.VMEM((count, piece, width), pieces.dtype),
-            pltpu.SMEM((count,), jnp.int32),
+            pltpu.SMEM(listing.shape, jnp.int32),
+            pltpu.VMEM((lines * len(smalls), 1, width), pieces.dtype),
+            pltpu.VMEM((owners, width), pieces.dtype),
             pltpu.SemaphoreType.DMA((steps,)),
             pltpu.SemaphoreType.DMA,
         ],
         compiler_params=ROOM,
         name="place_pieces",
-    )(slots, pieces, sums, notes)
-
-
-def pick_loop(which_ref, in_ref, out_ref, spots, stride):
+    )(listing, pieces, *smalls)
+
+
+def pick_loop(which_ref, in_ref, out_ref, spots, base_of):
     batch = 32
 
     def one(line, carry):
+        base = base_of(line)
         for first in range(0, len(spots), batch):
             rows = [in_ref[which_ref[line, k]] for k in range(first, first + batch)]
             for k in range(batch):
-                out_ref[line * stride + spots[first + k]] = rows[k]
+                out_ref[base + spots[first + k]] = rows[k]
         return carry
 
     lax.fori_loop(0, which_ref.shape[0], one, 0)
@@ -120,7 +134,7 @@
     width = rows.shape[2]
 
     def kernel(which_ref, in_ref, out_ref):
-        pick_loop(which_ref, in_ref, out_ref, range(lanes), lanes)
+        pick_loop(which_ref, in_ref, out_ref, range(lanes), lambda line: line * lanes)
 
     return pl.pallas_call(
         kernel,
@@ -132,7 +146,7 @@
     )(which, rows)
 
 
-def answer_and_join(got, which, blocks, spots, stride):
+def answer_and_join(got, which, blocks, spots, base_of):
     parts, _, piece, width = got.shape
 
     def kernel(which_ref, rows_ref, got_ref, out_ref, table_ref, sums_ref, left):
@@ -140,7 +154,7 @@
             pltpu.make_async_copy(got_ref.at[part, pl.ds(0, blocks)], table_ref.at[:, part], left).start()
         for part in range(parts):
             sums_ref[part] = got_ref[part, blocks]
-        pick_loop(which_ref, rows_ref, out_ref, spots, stride)
+        pick_loop(which_ref, rows_ref, out_ref, spots, base_of)
         pltpu.make_async_copy(table_ref, table_ref, left).wait()
 
     return pl.pallas_call(
@@ -165,7 +179,11 @@
     for by in range(1, peers):
         part = lax.dynamic_index_in_dim(parts, (me + by) % peers, 0, keepdims=False)
         held.append(lax.ppermute(part, axis, [(i, (i + by) % peers) for i in range(peers)]))
-    return jnp.stack(held)[(me - jnp.arange(peers)) % peers]
+    return held
+
+
+def line_of(group, shard):
+    return group // 2 * 128 + shard // 4 % 4 * 32 + shard // 16 * 8 + shard % 4 * 2 + group % 2
 
 
 def body(tables, accum, block_position, lookup_ids):
@@ -185,7 +203,9 @@
     spread, accum, block_position, lookup_ids = lax.optimization_barrier(
         (spread, accum, block_position, lookup_ids)
     )
-    pieces = lax.all_to_all(spread, both, split_axis=0, concat_axis=0, tiled=True)
+    pieces = lax.all_to_all(
+        spread.reshape(shards * groups, per_old, piece, width), ("dev", "grp"), split_axis=0, concat_axis=0, tiled=True
+    )
 
     table_ids = jnp.arange(table_count, dtype=jnp.int32)[None, :]
     id_place = block_position[table_ids, lookup_ids // TILE]
@@ -202,18 +222,7 @@
         .set(at_row)
     )
 
-    slot = ((table_grid * shards + owner) * limit + owner_order).reshape(-1, TILE)
-
-    small = jnp.concatenate(
-        [
-            accum.reshape(table_count, per_old, TILE),
-            asking.astype(jnp.float32).reshape(table_count, -1, TILE),
-        ],
-        axis=1,
-    )
-    small = swap_groups(small, "grp")
-    block_sums = small[:, :per_old].reshape(local, TILE)
-    passed = small[:, per_old:].reshape(groups, shards, limit)
+    slot = (line_of(table_grid, owner) * limit + owner_order).reshape(-1, TILE)
 
     counter = jnp.arange(local, dtype=jnp.int32)
     old_index = (counter // per_old * shards + my_shard) * per_old + counter % per_old
@@ -228,27 +237,43 @@
     slot_index = target * capacity + order_in
     source_of = jnp.zeros((shards * capacity,), jnp.int32).at[slot_index].set(counter)
     filled = jnp.zeros((shards * capacity,), jnp.int32).at[slot_index].set(1)
-    send_sums = block_sums[source_of].reshape(shards, capacity, TILE)
     send_place = jnp.where(filled == 1, slot_place[source_of], -1).reshape(shards, capacity)
-    notes = jnp.concatenate(
-        [passed.transpose(1, 0, 2).reshape(shards, groups * limit), send_place.astype(jnp.float32)], axis=1
-    )
-    notes = jnp.pad(notes[:, None, :], ((0, 0), (0, piece - 1), (0, TILE - notes.shape[1])))
-
+
+    asked = groups * limit
+    smalls = swap_groups(
+        jnp.concatenate(
+            [
+                accum.reshape(table_count, per_old, TILE),
+                lax.dynamic_update_slice(
+                    jnp.zeros((table_count, shards, TILE), jnp.float32),
+                    asking.astype(jnp.float32),
+                    (0, 0, my_group * limit),
+                ),
+            ],
+            axis=1,
+        ),
+        "grp",
+    )
+    smalls[0] = smalls[0] + jnp.pad(
+        send_place.astype(jnp.float32), ((per_old, 0), (asked, TILE - asked - capacity))
+    )
+    per_owner = local + 2
+    slots = (position_row + position_row // local * 2).reshape(groups, shards, per_old).transpose(1, 0, 2)
+    from_small = (my_group - source_of // per_old) % groups * per_old + source_of % per_old
+    listing = jnp.concatenate([slots.reshape(-1), from_small])
     pieces, slot = lax.optimization_barrier((pieces, slot))
 
-    slots = position_row + position_row // local * 2
     sending = place_pieces(
-        pieces.reshape(-1, piece, width), slots, send_sums, notes, shards * per_owner
+        pieces.reshape(-1, piece, width), listing, smalls, shards, shards * per_owner
     ).reshape(shards, per_owner, piece, width)
     got = lax.all_to_all(sending, "dev", split_axis=0, concat_axis=0, tiled=True)
 
-    asked = groups * limit
     got_notes = got[:, local + 1, 0].astype(jnp.int32)
-    spots = [(k // limit * shards) * limit + k % limit for k in range(asked)]
-    answer, new_table, got_sums = answer_and_join(got, got_notes, local, spots, limit)
+    spots = [line_of(k // limit, 0) * limit + k % limit for k in range(asked)]
+    answer, new_table, got_sums = answer_and_join(got, got_notes, local, spots, lambda shard: line_of(0, shard) * limit)
     answer = answer.reshape(groups * shards, limit, width)
-    returned = lax.all_to_all(answer, both, split_axis=0, concat_axis=0, tiled=True)
+    lines = sorted(range(groups * shards), key=lambda device: line_of(device // shards, device % shards))
+    returned = lax.all_to_all(answer, both, split_axis=0, concat_axis=0, axis_index_groups=[lines], tiled=True)
 
     new_table = new_table.reshape(1, local * TILE, width)
     got_sums, late_notes = lax.optimization_barrier((got_sums, got_notes))

time: 276 us -> 276 us (level)
    ppermute x3, waiting for transfers between devices: 64.9 us -> 1.65 us  [swap_groups(): lax.ppermute(part, axis, [(i, (i + by) % peers) for i in range(peers)])]
    all_to_all x2, waiting for transfers between devices: 28.8 us -> 90.5 us  [the longest x1 62.6 us: body(): lax.all_to_all(spread.reshape(shards * groups, per_old, piece, width), ('...]
where the time goes in v3:
time: 276 us; the launch traced here: 275 us
  blocking collectives  107 us (39%)
  waiting for transfers between devices  92.2 us (33%)
  starting transfers between devices  30.8 us (11%)
  local copies, waits for them, and re-layouts  24.7 us (9%)
  Pallas kernels  16 us (6%)
  other arithmetic  3.64 us (1%)
    all_to_all x1, blocking collectives, body(): lax.all_to_all(sending, 'dev', split_axis=0, concat_axis=0, tiled=True)  107 us
    all_to_all x1, waiting for transfers between devices, body(): lax.all_to_all(spread.reshape(shards * groups, per_old, piece, width), ('...  62.6 us
    all_to_all x1, waiting for transfers between devices, body(): lax.all_to_all(answer, both, split_axis=0, concat_axis=0, axis_index_grou...  28 us
    all_to_all x1, starting transfers between devices, body(): lax.all_to_all(spread.reshape(shards * groups, per_old, piece, width), ('...  16.7 us
    gather x5, local copies, waits for them, and re-layouts, body(): id_place = block_position[table_ids, lookup_ids // TILE]  9.54 us
    all_to_all x1, starting transfers between devices, body(): lax.all_to_all(answer, both, split_axis=0, concat_axis=0, axis_index_grou...  7.12 us
    ppermute x3, starting transfers between devices, swap_groups(): lax.ppermute(part, axis, [(i, (i + by) % peers) for i in range(peers)])  7.06 us
    pallas_call x1, Pallas kernels, place_pieces(): pl.pallas_call(kernel, in_specs=[HBM, HBM] + [VMEM] * len(smalls), out_sp...  5.77 us
  transfers between devices with their start and end apart: 5, of which 4 were waited for; matrix products, arithmetic and copies ran while one was open for 10% of the time, Pallas kernels for 0%

profile of v3, /device:TPU:1, one launch (start us, length us, event | category | flops | bytes accessed | tf_op | source)
XLA Modules:
  0.0 275.2 jit_solution(7050440816769760387)
XLA Ops:
  0.6 3.3 %spread_rows.1 = f32[64,4,16,2,128]{4,3,2,1,0:T(2,128)} custom-call(f32[4,16,64,2,128]{4,3,2,1,0:T(2,128)} %bitcast.121), custom_call_target="tpu_custom_call" | custom-call | tf_op jit(solution)/shard_map/spread_rows/pallas_call | solution.py:39
  3.9 16.7 %all-to-all-start = ((f32[256,16,2,128]{3,2,1,0:T(2,128)}), f32[256,16,2,128]{3,2,1,0:T(2,128)}, u32[]{:S(2)}, u32[]{:S(2)}) async-start(f32[256,16,2,128]{3,2,1,0:T(2,128)} %bitcast.120), calls=%async_computation | async-start | bytes 8388608 | tf_op jit(solution)/shard_map/all_to_all | solution.py:206
  20.9 9.1 %gather_fusion.1 = s32[1024]{0:T(1024)S(1)} fusion(s32[4,4096]{1,0:T(4,128)S(1)} %copy-done, s32[1024]{0:T(1024)S(1)} %reshape.360), kind=kCustom, calls=%fused_computation.1 | custom fusion | bytes 16384 | tf_op jit(solution)/shard_map/gather | solution.py:211
  30.7 2.4 reduce-window.6
  34.4 4.3 %scatter_custom_fusion.3 = s32[2048]{0:T(1024)S(1)} fusion(s32[1024]{0:T(1024)S(1)} %reshape.406, s32[1024]{0:T(1024)S(1)} %reshape.408, s32[]{:T(128)} %constant.247.clone.1), kind=kCustom, calls=%fused_computation.125 | custom fusion | bytes 8196
  39.0 1.0 dynamic_update_slice.3
  40.0 6.5 %collective-permute-start = (f32[80,128]{1,0:T(8,128)S(1)}, f32[80,128]{1,0:T(8,128)S(1)}, u32[]{:S(2)}, u32[]{:S(2)}) collective-permute-start(f32[80,128]{1,0:T(8,128)S(1)} %get-tuple-element.28), channel_id=1, source_target_pairs={{0,64},{64,128},{128,192},{192,0},{1,65},{65,129},{129,193},{193,1... | collective-permute-start | bytes 122888 | tf_op jit(solution)/shard_map/ppermute | solution.py:181
  46.6 0.4 collective-permute-start.1
  47.3 0.5 broadcast.704
  47.8 0.7 fusion.71
  48.5 0.8 gather_fusion
  49.6 0.8 scatter_custom_fusion
  50.4 0.8 scatter_custom_fusion.1
  51.3 1.2 gather_fusion.2
  54.1 62.6 %all-to-all-done = f32[256,16,2,128]{3,2,1,0:T(2,128)} async-done(((f32[256,16,2,128]{3,2,1,0:T(2,128)}), f32[256,16,2,128]{3,2,1,0:T(2,128)}, u32[]{:S(2)}, u32[]{:S(2)}) %all-to-all-start) | async-done | bytes 4194336 | tf_op jit(solution)/shard_map/all_to_all | solution.py:206
  116.6 1.4 collective-permute-done.1.refs_2_
  118.3 5.8 %place_pieces.1 = f32[4224,2,128]{2,1,0:T(2,128)S(1)} custom-call(s32[4224]{0:T(1024)S(1)} %pad_add_fusion.list_ref, f32[4096,2,128]{2,1,0:T(2,128)} %bitcast.13.in_ref, f32[80,128]{1,0:T(8,128)S(1)} %fusion.16.refs_0_, f32[80,128]{1,0:T(8,128)S(1)} %collective-permute-done.refs_1_, f32[80,128]{1,0:T(8,128)S(1)} %collective-permute-done.1.refs_2_, ...), custom_call_target="tpu_custom_call" | custom-call | tf_op jit(solution)/shard_map/place_pieces/pallas_call | solution.py:100
  124.1 106.6 %all_to_all.15.got_ref = f32[64,66,2,128]{3,2,1,0:T(2,128)S(1)} all-to-all(f32[64,66,2,128]{3,2,1,0:T(2,128)S(1)} %bitcast.114), channel_id=1, replica_groups=mesh['grp'=4,'dev'=64] {'dev'}, dimensions={0} | all-to-all | bytes 8650752 | tf_op jit(solution)/shard_map/all_to_all | solution.py:269
  230.7 4.8 %answer_and_join.1 = (f32[2048,1,128]{2,1,0:T(1,128)}, f32[64,64,2,128]{3,2,1,0:T(2,128)}, f32[64,2,128]{2,1,0:T(2,128)S(1)}) custom-call(s32[64,128]{1,0:T(8,128)S(1)} %bitcast.117, f32[8448,1,128]{2,1,0:T(1,128)S(1)} %bitcast.113, f32[64,66,2,128]{3,2,1,0:T(2,128)S(1)} %all_to_all.15.got_ref), custom_call_target="tpu_custom_call" | custom-call | tf_op jit(solution)/shard_map/answer_and_join/pallas_call | solution.py:160
  235.5 7.1 %all-to-all-start.2 = ((f32[256,8,128]{2,1,0:T(8,128)}), f32[256,8,128]{2,1,0:T(8,128)S(1)}, u32[]{:S(2)}, u32[]{:S(2)}) async-start(f32[256,8,128]{2,1,0:T(8,128)} %bitcast.28), calls=%async_computation.2 | async-start | bytes 2097152 | tf_op jit(solution)/shard_map/all_to_all | solution.py:276
  242.8 1.0 scatter_custom_fusion.2
  243.8 1.2 gather_fusion.3
  245.0 28.0 %all-to-all-done.2 = f32[256,8,128]{2,1,0:T(8,128)S(1)} async-done(((f32[256,8,128]{2,1,0:T(8,128)}), f32[256,8,128]{2,1,0:T(8,128)S(1)}, u32[]{:S(2)}, u32[]{:S(2)}) %all-to-all-start.2) | async-done | bytes 1048608 | tf_op jit(solution)/shard_map/all_to_all | solution.py:276
  273.0 2.2 pick_rows.1
  (89 shorter events, 5.0 us)
Async XLA Ops:
  3.9 16.7 %copy-start.2 = (s32[256,4]{0,1:T(4,128)S(1)}, s32[256,4]{0,1:T(4,128)}, u32[]{:S(2)}) copy-start(s32[256,4]{0,1:T(4,128)} %param.7) | copy-start | bytes 12292
  3.9 17.0 %copy-start = (s32[4,4096]{1,0:T(4,128)S(1)}, s32[4,4096]{1,0:T(4,128)}, u32[]{:S(2)}) copy-start(s32[4,4096]{1,0:T(4,128)} %param.6) | copy-start | bytes 196612
  3.9 112.7 %all-to-all-start = ((f32[256,16,2,128]{3,2,1,0:T(2,128)}), f32[256,16,2,128]{3,2,1,0:T(2,128)}, u32[]{:S(2)}, u32[]{:S(2)}) async-start(f32[256,16,2,128]{3,2,1,0:T(2,128)} %bitcast.120), calls=%async_computation | async-start | bytes 8388608 | tf_op jit(solution)/shard_map/all_to_all | solution.py:206
  20.9 12.8 %copy-start.4 = (s32[3]{0:T(128)S(1)}, s32[3]{0:T(128)}, u32[]{:S(2)}) copy-start(s32[3]{0:T(128)} %constant.269) | copy-start | bytes 40
  20.9 12.9 %copy-start.3 = (s32[3]{0:T(128)S(1)}, s32[3]{0:T(128)}, u32[]{:S(2)}) copy-start(s32[3]{0:T(128)} %constant.272) | copy-start | bytes 40
  20.9 18.0 %copy-start.1 = (f32[4,2048]{1,0:T(4,128)S(1)}, f32[4,2048]{1,0:T(4,128)}, u32[]{:S(2)}) copy-start(f32[4,2048]{1,0:T(4,128)} %param.5) | copy-start | bytes 98308
  40.0 76.6 %collective-permute-start = (f32[80,128]{1,0:T(8,128)S(1)}, f32[80,128]{1,0:T(8,128)S(1)}, u32[]{:S(2)}, u32[]{:S(2)}) collective-permute-start(f32[80,128]{1,0:T(8,128)S(1)} %get-tuple-element.28), channel_id=1, source_target_pairs={{0,64},{64,128},{128,192},{192,0},{1,65},{65,129},{129,193},{193,1... | collective-permute-start | bytes 122888 | tf_op jit(solution)/shard_map/ppermute | solution.py:181
  46.6 71.5 %collective-permute-start.1 = (f32[80,128]{1,0:T(8,128)S(1)}, f32[80,128]{1,0:T(8,128)S(1)}, u32[]{:S(2)}, u32[]{:S(2)}) collective-permute-start(f32[80,128]{1,0:T(8,128)S(1)} %get-tuple-element.29), channel_id=1, source_target_pairs={{0,128},{64,192},{128,0},{192,64},{1,129},{65,193},{129,1},{193,65... | collective-permute-start | bytes 122888 | tf_op jit(solution)/shard_map/ppermute | solution.py:181
  46.9 71.3 %collective-permute-start.2 = (f32[80,128]{1,0:T(8,128)S(1)}, f32[80,128]{1,0:T(8,128)S(1)}, u32[]{:S(2)}, u32[]{:S(2)}) collective-permute-start(f32[80,128]{1,0:T(8,128)S(1)} %get-tuple-element.27), channel_id=1, source_target_pairs={{0,192},{64,0},{128,64},{192,128},{1,193},{65,1},{129,65},{193,129... | collective-permute-start | bytes 122888 | tf_op jit(solution)/shard_map/ppermute | solution.py:181
  235.5 37.5 %all-to-all-start.2 = ((f32[256,8,128]{2,1,0:T(8,128)}), f32[256,8,128]{2,1,0:T(8,128)S(1)}, u32[]{:S(2)}, u32[]{:S(2)}) async-start(f32[256,8,128]{2,1,0:T(8,128)} %bitcast.28), calls=%async_computation.2 | async-start | bytes 2097152 | tf_op jit(solution)/shard_map/all_to_all | solution.py:276

commit v4 on v3

--- a/solution.py
+++ b/solution.py
@@ -50,17 +50,21 @@
     )(tables.reshape(count, blocks, parts, piece, width))
 
 
-def place_pieces(pieces, listing, smalls, owners, total):
+def place_pieces(pieces, listing, smalls, places_row, owners, total):
     count, piece, width = pieces.shape
+    groups = len(smalls)
     per_owner = total // owners
-    chunk = 512
-    steps = count // chunk
-    batch = 64
-    lines = smalls[0].shape[0] - owners
+    steps = 8
+    chunk = count // steps
+    batch = 32
+    lines = count // owners // groups
+    packed = smalls[0].shape[0] - lines
+    in_row = owners // packed
+    limit = width // in_row
 
     def kernel(list_ref, in_ref, *refs):
-        small_refs = refs[: len(smalls)]
-        out_ref, held, places, sums, notes, came, told = refs[len(smalls) :]
+        small_refs = refs[:groups]
+        row_ref, out_ref, held, places, sums, notes, came, told = refs[groups:]
 
         def fetch(step):
             span = pl.ds(step * chunk, chunk)
@@ -73,60 +77,57 @@
         for at, small_ref in enumerate(small_refs):
             for line in range(lines):
                 sums[at * lines + line] = small_ref[line : line + 1]
-        notes[...] = sum(small_ref[lines:] for small_ref in small_refs)
+        telling.wait()
+        lane_group = lax.broadcasted_iota(jnp.int32, (packed, width), 1) // limit
+        rows = [small_ref[lines:] for small_ref in small_refs]
+        senders = [(places[count + owners * piece] + groups - at) & (groups - 1) for at in range(groups)]
+        for at in range(in_row):
+            mixed = jnp.zeros((packed, width), pieces.dtype)
+            for sender, row in zip(senders, rows):
+                turn = (sender * limit + width - at * limit) & (width - 1)
+                mixed = jnp.where(lane_group == sender, pltpu.roll(row, turn, 1), mixed)
+            for line in range(packed):
+                notes[line * in_row + at : line * in_row + at + 1] = mixed[line : line + 1]
+        notes[...] = notes[...] + row_ref[...]
         for owner in range(owners):
             out_ref[owner * per_owner + per_owner - 1, 0:1] = notes[owner : owner + 1]
             out_ref[owner * per_owner + per_owner - 1, 1:2] = jnp.zeros((1, width), pieces.dtype)
-        telling.wait()
-        for owner in range(owners):
             for at in range(piece):
                 row = sums[places[count + owner * piece + at]]
                 out_ref[owner * per_owner + per_owner - 2, at : at + 1] = row
-
-        def one(step, carry):
+        for step in range(steps):
             fetch(step).wait()
-
-            def some(at, carry):
-                first = step * chunk + at * batch
-                rows = [held[first + k] for k in range(batch)]
+            for first in range(step * chunk, (step + 1) * chunk, batch):
+                some = [held[k] for k in range(first, first + batch)]
                 for k in range(batch):
-                    out_ref[places[first + k]] = rows[k]
-                return carry
-
-            return lax.fori_loop(0, chunk // batch, some, carry)
-
-        lax.fori_loop(0, steps, one, 0)
-
-    return pl.pallas_call(
-        kernel,
-        in_specs=[HBM, HBM] + [VMEM] * len(smalls),
+                    out_ref[places[first + k]] = some[k]
+
+    return pl.pallas_call(
+        kernel,
+        in_specs=[HBM, HBM] + [VMEM] * (groups + 1),
         out_specs=VMEM,
         out_shape=jax.ShapeDtypeStruct((total, piece, width), pieces.dtype),
         scratch_shapes=[
             pltpu.VMEM((count, piece, width), pieces.dtype),
             pltpu.SMEM(listing.shape, jnp.int32),
-            pltpu.VMEM((lines * len(smalls), 1, width), pieces.dtype),
+            pltpu.VMEM((lines * groups, 1, width), pieces.dtype),
             pltpu.VMEM((owners, width), pieces.dtype),
             pltpu.SemaphoreType.DMA((steps,)),
             pltpu.SemaphoreType.DMA,
         ],
         compiler_params=ROOM,
         name="place_pieces",
-    )(listing, pieces, *smalls)
-
-
-def pick_loop(which_ref, in_ref, out_ref, spots, base_of):
-    batch = 32
-
-    def one(line, carry):
-        base = base_of(line)
-        for first in range(0, len(spots), batch):
-            rows = [in_ref[which_ref[line, k]] for k in range(first, first + batch)]
-            for k in range(batch):
-                out_ref[base + spots[first + k]] = rows[k]
-        return carry
-
-    lax.fori_loop(0, which_ref.shape[0], one, 0)
+    )(listing, pieces, *smalls, places_row)
+
+
+def pick_all(which_ref, in_ref, out_ref, spot_of):
+    lines, _ = which_ref.shape
+    for line in range(lines):
+        for first in range(0, len(spot_of[line]), 32):
+            lanes = range(first, min(first + 32, len(spot_of[line])))
+            rows = [in_ref[which_ref[line, k]] for k in lanes]
+            for k, row in zip(lanes, rows):
+                out_ref[spot_of[line][k]] = row
 
 
 def pick_rows(rows, which):
@@ -134,7 +135,7 @@
     width = rows.shape[2]
 
     def kernel(which_ref, in_ref, out_ref):
-        pick_loop(which_ref, in_ref, out_ref, range(lanes), lambda line: line * lanes)
+        pick_all(which_ref, in_ref, out_ref, [range(line * lanes, (line + 1) * lanes) for line in range(lines)])
 
     return pl.pallas_call(
         kernel,
@@ -146,7 +147,7 @@
     )(which, rows)
 
 
-def answer_and_join(got, which, blocks, spots, base_of):
+def answer_and_join(got, which, blocks, spot_of):
     parts, _, piece, width = got.shape
 
     def kernel(which_ref, rows_ref, got_ref, out_ref, table_ref, sums_ref, left):
@@ -154,7 +155,7 @@
             pltpu.make_async_copy(got_ref.at[part, pl.ds(0, blocks)], table_ref.at[:, part], left).start()
         for part in range(parts):
             sums_ref[part] = got_ref[part, blocks]
-        pick_loop(which_ref, rows_ref, out_ref, spots, base_of)
+        pick_all(which_ref, rows_ref, out_ref, spot_of)
         pltpu.make_async_copy(table_ref, table_ref, left).wait()
 
     return pl.pallas_call(
@@ -162,7 +163,7 @@
         in_specs=[SMEM, VMEM, VMEM],
         out_specs=(VMEM, HBM, VMEM),
         out_shape=(
-            jax.ShapeDtypeStruct((parts * len(spots), 1, width), got.dtype),
+            jax.ShapeDtypeStruct((sum(map(len, spot_of)), 1, width), got.dtype),
             jax.ShapeDtypeStruct((blocks, parts, piece, width), got.dtype),
             jax.ShapeDtypeStruct((parts, piece, width), got.dtype),
         ),
@@ -239,38 +240,34 @@
     filled = jnp.zeros((shards * capacity,), jnp.int32).at[slot_index].set(1)
     send_place = jnp.where(filled == 1, slot_place[source_of], -1).reshape(shards, capacity)
 
-    asked = groups * limit
     smalls = swap_groups(
         jnp.concatenate(
             [
                 accum.reshape(table_count, per_old, TILE),
-                lax.dynamic_update_slice(
-                    jnp.zeros((table_count, shards, TILE), jnp.float32),
-                    asking.astype(jnp.float32),
-                    (0, 0, my_group * limit),
-                ),
+                asking.astype(jnp.float32).reshape(table_count, -1, TILE),
             ],
             axis=1,
         ),
         "grp",
     )
-    smalls[0] = smalls[0] + jnp.pad(
-        send_place.astype(jnp.float32), ((per_old, 0), (asked, TILE - asked - capacity))
-    )
+    asked = groups * limit
+    places_row = jnp.pad(send_place.astype(jnp.float32), ((0, 0), (asked, TILE - asked - capacity)))
     per_owner = local + 2
     slots = (position_row + position_row // local * 2).reshape(groups, shards, per_old).transpose(1, 0, 2)
     from_small = (my_group - source_of // per_old) % groups * per_old + source_of % per_old
-    listing = jnp.concatenate([slots.reshape(-1), from_small])
+    listing = jnp.concatenate([slots.reshape(-1), from_small, jnp.full((TILE,), my_group, jnp.int32)])
     pieces, slot = lax.optimization_barrier((pieces, slot))
 
     sending = place_pieces(
-        pieces.reshape(-1, piece, width), listing, smalls, shards, shards * per_owner
+        pieces.reshape(-1, piece, width), listing, smalls, places_row, shards, shards * per_owner
     ).reshape(shards, per_owner, piece, width)
     got = lax.all_to_all(sending, "dev", split_axis=0, concat_axis=0, tiled=True)
 
     got_notes = got[:, local + 1, 0].astype(jnp.int32)
-    spots = [line_of(k // limit, 0) * limit + k % limit for k in range(asked)]
-    answer, new_table, got_sums = answer_and_join(got, got_notes, local, spots, lambda shard: line_of(0, shard) * limit)
+    spot_of = [
+        [line_of(k // limit, shard) * limit + k % limit for k in range(asked)] for shard in range(shards)
+    ]
+    answer, new_table, got_sums = answer_and_join(got, got_notes, local, spot_of)
     answer = answer.reshape(groups * shards, limit, width)
     lines = sorted(range(groups * shards), key=lambda device: line_of(device // shards, device % shards))
     returned = lax.all_to_all(answer, both, split_axis=0, concat_axis=0, axis_index_groups=[lines], tiled=True)

time: 276 us -> 271 us (0.982)
  transfers between devices with their start and end apart: 5 -> 5, of which waited for: 4 -> 2; matrix products, arithmetic and copies ran while one was open for 10% -> 10% of each run, Pallas kernels for 0% -> 0%
where the time goes in v4:
time: 271 us; the launch traced here: 270 us
  blocking collectives  106 us (39%)
  waiting for transfers between devices  90.6 us (33%)
  starting transfers between devices  31.4 us (12%)
  local copies, waits for them, and re-layouts  24.1 us (9%)
  Pallas kernels  13.6 us (5%)
  other arithmetic  3.54 us (1%)
    all_to_all x1, blocking collectives, body(): lax.all_to_all(sending, 'dev', split_axis=0, concat_axis=0, tiled=True)  106 us
    all_to_all x1, waiting for transfers between devices, body(): lax.all_to_all(spread.reshape(shards * groups, per_old, piece, width), ('...  62.8 us
    all_to_all x1, waiting for transfers between devices, body(): lax.all_to_all(answer, both, split_axis=0, concat_axis=0, axis_index_grou...  27.8 us
    all_to_all x1, starting transfers between devices, body(): lax.all_to_all(spread.reshape(shards * groups, per_old, piece, width), ('...  16.7 us
    gather x5, local copies, waits for them, and re-layouts, body(): id_place = block_position[table_ids, lookup_ids // TILE]  9.54 us
    ppermute x3, starting transfers between devices, swap_groups(): lax.ppermute(part, axis, [(i, (i + by) % peers) for i in range(peers)])  7.56 us
    all_to_all x1, starting transfers between devices, body(): lax.all_to_all(answer, both, split_axis=0, concat_axis=0, axis_index_grou...  7.23 us
  transfers between devices with their start and end apart: 5, of which 2 were waited for; matrix products, arithmetic and copies ran while one was open for 10% of the time, Pallas kernels for 0%

profile of v4, /device:TPU:1, one launch (start us, length us, event | category | flops | bytes accessed | tf_op | source)
XLA Modules:
  0.0 270.4 jit_solution(13559089554576295467)
XLA Ops:
  0.6 3.3 %spread_rows.1 = f32[64,4,16,2,128]{4,3,2,1,0:T(2,128)} custom-call(f32[4,16,64,2,128]{4,3,2,1,0:T(2,128)} %bitcast.118), custom_call_target="tpu_custom_call" | custom-call | tf_op jit(solution)/shard_map/spread_rows/pallas_call | solution.py:39
  3.9 16.7 %all-to-all-start = ((f32[256,16,2,128]{3,2,1,0:T(2,128)}), f32[256,16,2,128]{3,2,1,0:T(2,128)}, u32[]{:S(2)}, u32[]{:S(2)}) async-start(f32[256,16,2,128]{3,2,1,0:T(2,128)} %bitcast.117), calls=%async_computation | async-start | bytes 8388608 | tf_op jit(solution)/shard_map/all_to_all | solution.py:207
  20.9 9.1 %gather_fusion.1 = s32[1024]{0:T(1024)S(1)} fusion(s32[4,4096]{1,0:T(4,128)S(1)} %copy-done, s32[1024]{0:T(1024)S(1)} %reshape.364), kind=kCustom, calls=%fused_computation.1 | custom fusion | bytes 16384 | tf_op jit(solution)/shard_map/gather | solution.py:212
  30.7 2.4 reduce-window.6
  33.1 0.3 slice_reduce_fusion
  34.4 4.3 %scatter_custom_fusion.3 = s32[2048]{0:T(1024)S(1)} fusion(s32[1024]{0:T(1024)S(1)} %reshape.410, s32[1024]{0:T(1024)S(1)} %reshape.412, s32[]{:T(128)} %constant.245.clone.1), kind=kCustom, calls=%fused_computation.113 | custom fusion | bytes 8196
  39.1 6.5 %collective-permute-start = (f32[20,128]{1,0:T(8,128)S(1)}, f32[20,128]{1,0:T(8,128)S(1)}, u32[]{:S(2)}, u32[]{:S(2)}) collective-permute-start(f32[20,128]{1,0:T(8,128)S(1)} %get-tuple-element.29), channel_id=1, source_target_pairs={{0,64},{64,128},{128,192},{192,0},{1,65},{65,129},{129,193},{193,1... | collective-permute-start | bytes 30728 | tf_op jit(solution)/shard_map/ppermute | solution.py:182
  45.7 1.0 collective-permute-start.1
  46.9 0.5 broadcast.704
  47.4 0.7 fusion.62
  48.1 0.8 gather_fusion
  49.0 0.2 select_reduce_fusion
  49.3 0.8 scatter_custom_fusion
  50.1 1.0 scatter_custom_fusion.1
  52.4 1.2 gather_fusion.2
  53.9 62.8 %all-to-all-done = f32[256,16,2,128]{3,2,1,0:T(2,128)} async-done(((f32[256,16,2,128]{3,2,1,0:T(2,128)}), f32[256,16,2,128]{3,2,1,0:T(2,128)}, u32[]{:S(2)}, u32[]{:S(2)}) %all-to-all-start) | async-done | bytes 4194336 | tf_op jit(solution)/shard_map/all_to_all | solution.py:207
  116.6 4.4 %place_pieces.1 = f32[4224,2,128]{2,1,0:T(2,128)S(1)} custom-call(s32[4352]{0:T(1024)S(1)} %pad_add_fusion.list_ref, f32[4096,2,128]{2,1,0:T(2,128)} %bitcast.13.in_ref, f32[20,128]{1,0:T(8,128)S(1)} %get-tuple-element.30.refs_0_, f32[20,128]{1,0:T(8,128)S(1)} %collective-permute-done.refs_1_, f32[20,128]{1,0:T(8,128)S(1)} %collective-permute-done.1.refs_2_, ...), custom_call_target="tpu_custom_call" | custom-call | tf_op jit(solution)/shard_map/place_pieces/pallas_call | solution.py:105
  121.0 105.9 %all_to_all.15.got_ref = f32[64,66,2,128]{3,2,1,0:T(2,128)S(1)} all-to-all(f32[64,66,2,128]{3,2,1,0:T(2,128)S(1)} %bitcast.111), channel_id=1, replica_groups=mesh['grp'=4,'dev'=64] {'dev'}, dimensions={0} | all-to-all | bytes 8650752 | tf_op jit(solution)/shard_map/all_to_all | solution.py:264
  226.9 4.0 %answer_and_join.1 = (f32[2048,1,128]{2,1,0:T(1,128)}, f32[64,64,2,128]{3,2,1,0:T(2,128)}, f32[64,2,128]{2,1,0:T(2,128)S(1)}) custom-call(s32[64,128]{1,0:T(8,128)S(1)} %bitcast.114, f32[8448,1,128]{2,1,0:T(1,128)S(1)} %bitcast.110, f32[64,66,2,128]{3,2,1,0:T(2,128)S(1)} %all_to_all.15.got_ref), custom_call_target="tpu_custom_call" | custom-call | tf_op jit(solution)/shard_map/answer_and_join/pallas_call | solution.py:161
  231.0 7.2 %all-to-all-start.2 = ((f32[256,8,128]{2,1,0:T(8,128)}), f32[256,8,128]{2,1,0:T(8,128)S(1)}, u32[]{:S(2)}, u32[]{:S(2)}) async-start(f32[256,8,128]{2,1,0:T(8,128)} %bitcast.28), calls=%async_computation.2 | async-start | bytes 2097152 | tf_op jit(solution)/shard_map/all_to_all | solution.py:273
  238.5 1.0 scatter_custom_fusion.2
  239.5 1.2 gather_fusion.3
  240.7 27.8 %all-to-all-done.2 = f32[256,8,128]{2,1,0:T(8,128)S(1)} async-done(((f32[256,8,128]{2,1,0:T(8,128)}), f32[256,8,128]{2,1,0:T(8,128)S(1)}, u32[]{:S(2)}, u32[]{:S(2)}) %all-to-all-start.2) | async-done | bytes 1048608 | tf_op jit(solution)/shard_map/all_to_all | solution.py:273
  268.5 1.9 pick_rows.1
  (90 shorter events, 4.2 us)
Async XLA Ops:
  3.9 16.7 %copy-start.2 = (s32[256,4]{0,1:T(4,128)S(1)}, s32[256,4]{0,1:T(4,128)}, u32[]{:S(2)}) copy-start(s32[256,4]{0,1:T(4,128)} %param.7) | copy-start | bytes 12292
  3.9 17.0 %copy-start = (s32[4,4096]{1,0:T(4,128)S(1)}, s32[4,4096]{1,0:T(4,128)}, u32[]{:S(2)}) copy-start(s32[4,4096]{1,0:T(4,128)} %param.6) | copy-start | bytes 196612
  3.9 112.7 %all-to-all-start = ((f32[256,16,2,128]{3,2,1,0:T(2,128)}), f32[256,16,2,128]{3,2,1,0:T(2,128)}, u32[]{:S(2)}, u32[]{:S(2)}) async-start(f32[256,16,2,128]{3,2,1,0:T(2,128)} %bitcast.117), calls=%async_computation | async-start | bytes 8388608 | tf_op jit(solution)/shard_map/all_to_all | solution.py:207
  20.9 12.8 %copy-start.4 = (s32[3]{0:T(128)S(1)}, s32[3]{0:T(128)}, u32[]{:S(2)}) copy-start(s32[3]{0:T(128)} %constant.267) | copy-start | bytes 40
  20.9 12.9 %copy-start.3 = (s32[3]{0:T(128)S(1)}, s32[3]{0:T(128)}, u32[]{:S(2)}) copy-start(s32[3]{0:T(128)} %constant.270) | copy-start | bytes 40
  20.9 18.2 %copy-start.1 = (f32[4,2048]{1,0:T(4,128)S(1)}, f32[4,2048]{1,0:T(4,128)}, u32[]{:S(2)}) copy-start(f32[4,2048]{1,0:T(4,128)} %param.5) | copy-start | bytes 98308
  39.1 77.5 %collective-permute-start = (f32[20,128]{1,0:T(8,128)S(1)}, f32[20,128]{1,0:T(8,128)S(1)}, u32[]{:S(2)}, u32[]{:S(2)}) collective-permute-start(f32[20,128]{1,0:T(8,128)S(1)} %get-tuple-element.29), channel_id=1, source_target_pairs={{0,64},{64,128},{128,192},{192,0},{1,65},{65,129},{129,193},{193,1... | collective-permute-start | bytes 30728 | tf_op jit(solution)/shard_map/ppermute | solution.py:182
  45.7 70.9 %collective-permute-start.1 = (f32[20,128]{1,0:T(8,128)S(1)}, f32[20,128]{1,0:T(8,128)S(1)}, u32[]{:S(2)}, u32[]{:S(2)}) collective-permute-start(f32[20,128]{1,0:T(8,128)S(1)} %get-tuple-element.28), channel_id=1, source_target_pairs={{0,128},{64,192},{128,0},{192,64},{1,129},{65,193},{129,1},{193,65... | collective-permute-start | bytes 30728 | tf_op jit(solution)/shard_map/ppermute | solution.py:182
  46.7 69.9 %collective-permute-start.2 = (f32[20,128]{1,0:T(8,128)S(1)}, f32[20,128]{1,0:T(8,128)S(1)}, u32[]{:S(2)}, u32[]{:S(2)}) collective-permute-start(f32[20,128]{1,0:T(8,128)S(1)} %get-tuple-element.27), channel_id=1, source_target_pairs={{0,192},{64,0},{128,64},{192,128},{1,193},{65,1},{129,65},{193,129... | collective-permute-start | bytes 30728 | tf_op jit(solution)/shard_map/ppermute | solution.py:182
  231.0 37.5 %all-to-all-start.2 = ((f32[256,8,128]{2,1,0:T(8,128)}), f32[256,8,128]{2,1,0:T(8,128)S(1)}, u32[]{:S(2)}, u32[]{:S(2)}) async-start(f32[256,8,128]{2,1,0:T(8,128)} %bitcast.28), calls=%async_computation.2 | async-start | bytes 2097152 | tf_op jit(solution)/shard_map/all_to_all | solution.py:273

commit v5 on v4

--- a/solution.py
+++ b/solution.py
@@ -149,25 +149,37 @@
 
 def answer_and_join(got, which, blocks, spot_of):
     parts, _, piece, width = got.shape
-
-    def kernel(which_ref, rows_ref, got_ref, out_ref, table_ref, sums_ref, left):
+    asked = len(spot_of[0])
+
+    def kernel(list_ref, rows_ref, got_ref, out_ref, table_ref, sums_ref, which_ref, sums, told, left):
+        telling = pltpu.make_async_copy(list_ref, which_ref, told)
+        telling.start()
         for part in range(parts):
             pltpu.make_async_copy(got_ref.at[part, pl.ds(0, blocks)], table_ref.at[:, part], left).start()
+        telling.wait()
+        pick_all(which_ref, rows_ref, out_ref, spot_of)
         for part in range(parts):
-            sums_ref[part] = got_ref[part, blocks]
-        pick_all(which_ref, rows_ref, out_ref, spot_of)
+            for at in range(piece):
+                sums[which_ref[part, asked + at]] = got_ref[part, blocks, at : at + 1]
+        for block in range(blocks):
+            sums_ref[block] = sums[block]
         pltpu.make_async_copy(table_ref, table_ref, left).wait()
 
     return pl.pallas_call(
         kernel,
-        in_specs=[SMEM, VMEM, VMEM],
+        in_specs=[HBM, VMEM, VMEM],
         out_specs=(VMEM, HBM, VMEM),
         out_shape=(
             jax.ShapeDtypeStruct((sum(map(len, spot_of)), 1, width), got.dtype),
             jax.ShapeDtypeStruct((blocks, parts, piece, width), got.dtype),
-            jax.ShapeDtypeStruct((parts, piece, width), got.dtype),
+            jax.ShapeDtypeStruct((blocks, 1, width), got.dtype),
         ),
-        scratch_shapes=[pltpu.SemaphoreType.DMA],
+        scratch_shapes=[
+            pltpu.SMEM(which.shape, jnp.int32),
+            pltpu.VMEM((blocks + 1, 1, width), got.dtype),
+            pltpu.SemaphoreType.DMA,
+            pltpu.SemaphoreType.DMA,
+        ],
         compiler_params=ROOM,
         name="answer_and_join",
     )(which, got.reshape(-1, 1, width), got)
@@ -238,7 +250,7 @@
     slot_index = target * capacity + order_in
     source_of = jnp.zeros((shards * capacity,), jnp.int32).at[slot_index].set(counter)
     filled = jnp.zeros((shards * capacity,), jnp.int32).at[slot_index].set(1)
-    send_place = jnp.where(filled == 1, slot_place[source_of], -1).reshape(shards, capacity)
+    send_place = jnp.where(filled == 1, slot_place[source_of], local).reshape(shards, capacity)
 
     smalls = swap_groups(
         jnp.concatenate(
@@ -267,21 +279,13 @@
     spot_of = [
         [line_of(k // limit, shard) * limit + k % limit for k in range(asked)] for shard in range(shards)
     ]
-    answer, new_table, got_sums = answer_and_join(got, got_notes, local, spot_of)
+    answer, new_table, new_sums = answer_and_join(got, got_notes, local, spot_of)
     answer = answer.reshape(groups * shards, limit, width)
     lines = sorted(range(groups * shards), key=lambda device: line_of(device // shards, device % shards))
     returned = lax.all_to_all(answer, both, split_axis=0, concat_axis=0, axis_index_groups=[lines], tiled=True)
 
     new_table = new_table.reshape(1, local * TILE, width)
-    got_sums, late_notes = lax.optimization_barrier((got_sums, got_notes))
-    flat_place = late_notes[:, asked : asked + capacity].reshape(-1)
-    landing = jnp.where(flat_place >= 0, flat_place, local)
-    picker = (
-        jnp.zeros((local,), jnp.int32)
-        .at[landing]
-        .set(jnp.arange(shards * capacity, dtype=jnp.int32), mode="drop")
-    )
-    new_accum = got_sums.reshape(shards * capacity, TILE)[picker].reshape(1, local * TILE)
+    new_accum = new_sums.reshape(1, local * TILE)
 
     looked = pick_rows(returned.reshape(-1, 1, width), slot)
     looked = looked.reshape(look_rows, table_count, width)

time: 271 us -> 270 us (level)
  blocking collectives: 106 us -> 143 us
  waiting for transfers between devices: 90.6 us -> 58.1 us
    all_to_all x0 -> x1, blocking collectives: none -> 37.7 us  [body(): lax.all_to_all(answer, both, split_axis=0, concat_axis=0, axis_index_grou...]
    all_to_all x1 -> x0, waiting for transfers between devices: 27.8 us -> none  [body(): lax.all_to_all(answer, both, split_axis=0, concat_axis=0, axis_index_grou...]
    all_to_all x1 -> x0, starting transfers between devices: 7.23 us -> none  [body(): lax.all_to_all(answer, both, split_axis=0, concat_axis=0, axis_index_grou...]
    ppermute x3, starting transfers between devices: 7.56 us -> 12.2 us  [swap_groups(): lax.ppermute(part, axis, [(i, (i + by) % peers) for i in range(peers)])]
    all_to_all x1, waiting for transfers between devices: 62.8 us -> 58.1 us  [body(): lax.all_to_all(spread.reshape(shards * groups, per_old, piece, width), ('...]
  transfers between devices with their start and end apart: 5 -> 4, of which waited for: 2 -> 1; matrix products, arithmetic and copies ran while one was open for 10% -> 9% of each run, Pallas kernels for 0% -> 0%
where the time goes in v5:
time: 270 us; the launch traced here: 269 us
  blocking collectives  143 us (53%)
  waiting for transfers between devices  58.1 us (22%)
  starting transfers between devices  28.9 us (11%)
  local copies, waits for them, and re-layouts  21.7 us (8%)
  Pallas kernels  12.5 us (5%)
  other arithmetic  3.53 us (1%)
    all_to_all x1, blocking collectives, body(): lax.all_to_all(sending, 'dev', split_axis=0, concat_axis=0, tiled=True)  106 us
    all_to_all x1, waiting for transfers between devices, body(): lax.all_to_all(spread.reshape(shards * groups, per_old, piece, width), ('...  58.1 us
    all_to_all x1, blocking collectives, body(): lax.all_to_all(answer, both, split_axis=0, concat_axis=0, axis_index_grou...  37.7 us
    all_to_all x1, starting transfers between devices, body(): lax.all_to_all(spread.reshape(shards * groups, per_old, piece, width), ('...  16.7 us
    ppermute x3, starting transfers between devices, swap_groups(): lax.ppermute(part, axis, [(i, (i + by) % peers) for i in range(peers)])  12.2 us
    gather x5, local copies, waits for them, and re-layouts, body(): id_place = block_position[table_ids, lookup_ids // TILE]  9.54 us
  transfers between devices with their start and end apart: 4, of which 1 were waited for; matrix products, arithmetic and copies ran while one was open for 9% of the time, Pallas kernels for 0%

profile of v5, /device:TPU:1, one launch (start us, length us, event | category | flops | bytes accessed | tf_op | source)
XLA Modules:
  0.0 269.3 jit_solution(17543903147151353209)
XLA Ops:
  0.6 3.3 %spread_rows.1 = f32[64,4,16,2,128]{4,3,2,1,0:T(2,128)} custom-call(f32[4,16,64,2,128]{4,3,2,1,0:T(2,128)} %bitcast.117), custom_call_target="tpu_custom_call" | custom-call | tf_op jit(solution)/shard_map/spread_rows/pallas_call | solution.py:39
  3.9 16.7 %all-to-all-start = ((f32[256,16,2,128]{3,2,1,0:T(2,128)}), f32[256,16,2,128]{3,2,1,0:T(2,128)}, u32[]{:S(2)}, u32[]{:S(2)}) async-start(f32[256,16,2,128]{3,2,1,0:T(2,128)} %bitcast.116), calls=%async_computation | async-start | bytes 8388608 | tf_op jit(solution)/shard_map/all_to_all | solution.py:219
  21.0 9.1 %gather_fusion.1 = s32[1024]{0:T(1024)S(1)} fusion(s32[4,4096]{1,0:T(4,128)S(1)} %copy-done, s32[1024]{0:T(1024)S(1)} %reshape.328), kind=kCustom, calls=%fused_computation.1 | custom fusion | bytes 16384 | tf_op jit(solution)/shard_map/gather | solution.py:224
  31.0 2.4 reduce-window.6
  33.4 0.3 slice_reduce_fusion
  33.8 0.2 fusion.2
  34.2 0.1 copy.37
  34.4 4.3 %scatter_custom_fusion.2 = s32[2048]{0:T(1024)S(1)} fusion(s32[1024]{0:T(1024)S(1)} %reshape.358, s32[1024]{0:T(1024)S(1)} %reshape.360, s32[]{:T(128)} %constant.244.clone.1), kind=kCustom, calls=%fused_computation.110 | custom fusion | bytes 8196
  39.1 2.3 collective-permute-start.2
  41.4 4.4 %collective-permute-start.1 = (f32[20,128]{1,0:T(8,128)S(1)}, f32[20,128]{1,0:T(8,128)S(1)}, u32[]{:S(2)}, u32[]{:S(2)}) collective-permute-start(f32[20,128]{1,0:T(8,128)S(1)} %get-tuple-element.24), channel_id=1, source_target_pairs={{0,128},{64,192},{128,0},{192,64},{1,129},{65,193},{129,1},{193,65... | collective-permute-start | bytes 30728 | tf_op jit(solution)/shard_map/ppermute | solution.py:194
  45.8 5.5 %collective-permute-start = (f32[20,128]{1,0:T(8,128)S(1)}, f32[20,128]{1,0:T(8,128)S(1)}, u32[]{:S(2)}, u32[]{:S(2)}) collective-permute-start(f32[20,128]{1,0:T(8,128)S(1)} %get-tuple-element.25), channel_id=1, source_target_pairs={{0,64},{64,128},{128,192},{192,0},{1,65},{65,129},{129,193},{193,1... | collective-permute-start | bytes 30728 | tf_op jit(solution)/shard_map/ppermute | solution.py:194
  52.3 0.5 broadcast.654
  52.8 0.7 fusion.59
  53.5 0.8 gather_fusion
  54.5 0.2 select_reduce_fusion
  54.7 0.8 scatter_custom_fusion.1
  55.5 1.0 scatter_custom_fusion
  57.0 1.2 gather_fusion.2
  58.5 58.1 %all-to-all-done = f32[256,16,2,128]{3,2,1,0:T(2,128)} async-done(((f32[256,16,2,128]{3,2,1,0:T(2,128)}), f32[256,16,2,128]{3,2,1,0:T(2,128)}, u32[]{:S(2)}, u32[]{:S(2)}) %all-to-all-start) | async-done | bytes 4194336 | tf_op jit(solution)/shard_map/all_to_all | solution.py:219
  116.6 4.4 %place_pieces.1 = f32[4224,2,128]{2,1,0:T(2,128)S(1)} custom-call(s32[4352]{0:T(1024)S(1)} %pad_add_fusion.list_ref, f32[4096,2,128]{2,1,0:T(2,128)} %bitcast.13.in_ref, f32[20,128]{1,0:T(8,128)S(1)} %get-tuple-element.26.refs_0_, f32[20,128]{1,0:T(8,128)S(1)} %collective-permute-done.refs_1_, f32[20,128]{1,0:T(8,128)S(1)} %collective-permute-done.1.refs_2_, ...), custom_call_target="tpu_custom_call" | custom-call | tf_op jit(solution)/shard_map/place_pieces/pallas_call | solution.py:105
  121.0 105.7 %all_to_all.15.got_ref = f32[64,66,2,128]{3,2,1,0:T(2,128)S(1)} all-to-all(f32[64,66,2,128]{3,2,1,0:T(2,128)S(1)} %bitcast.111), channel_id=1, replica_groups=mesh['grp'=4,'dev'=64] {'dev'}, dimensions={0} | all-to-all | bytes 8650752 | tf_op jit(solution)/shard_map/all_to_all | solution.py:276
  226.7 2.9 %answer_and_join.1 = (f32[2048,1,128]{2,1,0:T(1,128)S(1)}, f32[64,64,2,128]{3,2,1,0:T(2,128)}, f32[64,1,128]{2,1,0:T(1,128)}) custom-call(s32[64,128]{1,0:T(8,128)S(1)} %bitcast.114, f32[8448,1,128]{2,1,0:T(1,128)S(1)} %bitcast.110, f32[64,66,2,128]{3,2,1,0:T(2,128)S(1)} %all_to_all.15.got_ref), custom_call_target="tpu_custom_call" | custom-call | tf_op jit(solution)/shard_map/answer_and_join/pallas_call | solution.py:168
  229.7 37.7 %all_to_all.16 = f32[256,8,128]{2,1,0:T(8,128)S(1)} all-to-all(f32[256,8,128]{2,1,0:T(8,128)S(1)} %bitcast.113), channel_id=1, replica_groups={{0,64,1,65,2,66,3,67,16,80,17,81,18,82,19,83,32,96,33,97,34,98,35,99,48..., dimensions={0} | all-to-all | bytes 2097152 | tf_op jit(solution)/shard_map/all_to_all | solution.py:285
  267.3 1.9 pick_rows.1
  (81 shorter events, 3.7 us)
Async XLA Ops:
  3.9 16.7 %copy-start.2 = (s32[256,4]{0,1:T(4,128)S(1)}, s32[256,4]{0,1:T(4,128)}, u32[]{:S(2)}) copy-start(s32[256,4]{0,1:T(4,128)} %param.7) | copy-start | bytes 12292
  3.9 17.0 %copy-start = (s32[4,4096]{1,0:T(4,128)S(1)}, s32[4,4096]{1,0:T(4,128)}, u32[]{:S(2)}) copy-start(s32[4,4096]{1,0:T(4,128)} %param.6) | copy-start | bytes 196612
  3.9 112.7 %all-to-all-start = ((f32[256,16,2,128]{3,2,1,0:T(2,128)}), f32[256,16,2,128]{3,2,1,0:T(2,128)}, u32[]{:S(2)}, u32[]{:S(2)}) async-start(f32[256,16,2,128]{3,2,1,0:T(2,128)} %bitcast.116), calls=%async_computation | async-start | bytes 8388608 | tf_op jit(solution)/shard_map/all_to_all | solution.py:219
  20.9 13.1 %copy-start.4 = (s32[3]{0:T(128)S(1)}, s32[3]{0:T(128)}, u32[]{:S(2)}) copy-start(s32[3]{0:T(128)} %constant.266) | copy-start | bytes 40
  20.9 13.1 %copy-start.3 = (s32[3]{0:T(128)S(1)}, s32[3]{0:T(128)}, u32[]{:S(2)}) copy-start(s32[3]{0:T(128)} %constant.269) | copy-start | bytes 40
  20.9 18.1 %copy-start.1 = (f32[4,2048]{1,0:T(4,128)S(1)}, f32[4,2048]{1,0:T(4,128)}, u32[]{:S(2)}) copy-start(f32[4,2048]{1,0:T(4,128)} %param.5) | copy-start | bytes 98308
  39.1 77.5 %collective-permute-start.2 = (f32[20,128]{1,0:T(8,128)S(1)}, f32[20,128]{1,0:T(8,128)S(1)}, u32[]{:S(2)}, u32[]{:S(2)}) collective-permute-start(f32[20,128]{1,0:T(8,128)S(1)} %get-tuple-element.23), channel_id=1, source_target_pairs={{0,192},{64,0},{128,64},{192,128},{1,193},{65,1},{129,65},{193,129... | collective-permute-start | bytes 30728 | tf_op jit(solution)/shard_map/ppermute | solution.py:194
  41.4 75.2 %collective-permute-start.1 = (f32[20,128]{1,0:T(8,128)S(1)}, f32[20,128]{1,0:T(8,128)S(1)}, u32[]{:S(2)}, u32[]{:S(2)}) collective-permute-start(f32[20,128]{1,0:T(8,128)S(1)} %get-tuple-element.24), channel_id=1, source_target_pairs={{0,128},{64,192},{128,0},{192,64},{1,129},{65,193},{129,1},{193,65... | collective-permute-start | bytes 30728 | tf_op jit(solution)/shard_map/ppermute | solution.py:194
  45.8 70.8 %collective-permute-start = (f32[20,128]{1,0:T(8,128)S(1)}, f32[20,128]{1,0:T(8,128)S(1)}, u32[]{:S(2)}, u32[]{:S(2)}) collective-permute-start(f32[20,128]{1,0:T(8,128)S(1)} %get-tuple-element.25), channel_id=1, source_target_pairs={{0,64},{64,128},{128,192},{192,0},{1,65},{65,129},{129,193},{193,1... | collective-permute-start | bytes 30728 | tf_op jit(solution)/shard_map/ppermute | solution.py:194

commit v6 on v5

--- a/solution.py
+++ b/solution.py
@@ -130,32 +130,50 @@
                 out_ref[spot_of[line][k]] = row
 
 
-def pick_rows(rows, which):
+def join_some(got_ref, table_ref, parts, left):
+    blocks = table_ref.shape[0]
+    for part in parts:
+        pltpu.make_async_copy(got_ref.at[part, pl.ds(0, blocks)], table_ref.at[:, part], left).start()
+    some = table_ref.at[:, pl.ds(parts[0], len(parts))]
+    return pltpu.make_async_copy(some, some, left)
+
+
+def look_and_join(returned, which, got, table, done):
     lines, lanes = which.shape
-    width = rows.shape[2]
-
-    def kernel(which_ref, in_ref, out_ref):
-        pick_all(which_ref, in_ref, out_ref, [range(line * lanes, (line + 1) * lanes) for line in range(lines)])
+    width = returned.shape[2]
+    parts = got.shape[0]
+
+    def kernel(list_ref, rows_ref, got_ref, _, out_ref, table_ref, which_ref, told, left):
+        telling = pltpu.make_async_copy(list_ref, which_ref, told)
+        telling.start()
+        joining = join_some(got_ref, table_ref, range(done, parts), left)
+        telling.wait()
+        pick_all(which_ref, rows_ref, out_ref, [range(line * lanes, (line + 1) * lanes) for line in range(lines)])
+        joining.wait()
 
     return pl.pallas_call(
         kernel,
-        in_specs=[SMEM, VMEM],
-        out_specs=VMEM,
-        out_shape=jax.ShapeDtypeStruct((lines * lanes, 1, width), rows.dtype),
+        in_specs=[HBM, VMEM, VMEM, HBM],
+        out_specs=(VMEM, HBM),
+        out_shape=(
+            jax.ShapeDtypeStruct((lines * lanes, 1, width), returned.dtype),
+            jax.ShapeDtypeStruct(table.shape, table.dtype),
+        ),
+        input_output_aliases={3: 1},
+        scratch_shapes=[pltpu.SMEM(which.shape, jnp.int32), pltpu.SemaphoreType.DMA, pltpu.SemaphoreType.DMA],
         compiler_params=ROOM,
-        name="pick_rows",
-    )(which, rows)
-
-
-def answer_and_join(got, which, blocks, spot_of):
+        name="look_and_join",
+    )(which, returned, got, table)
+
+
+def answer_and_join(got, which, blocks, spot_of, done):
     parts, _, piece, width = got.shape
     asked = len(spot_of[0])
 
     def kernel(list_ref, rows_ref, got_ref, out_ref, table_ref, sums_ref, which_ref, sums, told, left):
         telling = pltpu.make_async_copy(list_ref, which_ref, told)
         telling.start()
-        for part in range(parts):
-            pltpu.make_async_copy(got_ref.at[part, pl.ds(0, blocks)], table_ref.at[:, part], left).start()
+        joining = join_some(got_ref, table_ref, range(done), left)
         telling.wait()
         pick_all(which_ref, rows_ref, out_ref, spot_of)
         for part in range(parts):
@@ -163,7 +181,7 @@
                 sums[which_ref[part, asked + at]] = got_ref[part, blocks, at : at + 1]
         for block in range(blocks):
             sums_ref[block] = sums[block]
-        pltpu.make_async_copy(table_ref, table_ref, left).wait()
+        joining.wait()
 
     return pl.pallas_call(
         kernel,
@@ -279,16 +297,16 @@
     spot_of = [
         [line_of(k // limit, shard) * limit + k % limit for k in range(asked)] for shard in range(shards)
     ]
-    answer, new_table, new_sums = answer_and_join(got, got_notes, local, spot_of)
+    joined = shards * 5 // 8
+    answer, new_table, new_sums = answer_and_join(got, got_notes, local, spot_of, joined)
     answer = answer.reshape(groups * shards, limit, width)
     lines = sorted(range(groups * shards), key=lambda device: line_of(device // shards, device % shards))
     returned = lax.all_to_all(answer, both, split_axis=0, concat_axis=0, axis_index_groups=[lines], tiled=True)
 
+    looked, new_table = look_and_join(returned.reshape(-1, 1, width), slot, got, new_table, joined)
+    looked = looked.reshape(look_rows, table_count, width)
     new_table = new_table.reshape(1, local * TILE, width)
     new_accum = new_sums.reshape(1, local * TILE)
-
-    looked = pick_rows(returned.reshape(-1, 1, width), slot)
-    looked = looked.reshape(look_rows, table_count, width)
     return (new_table, new_accum, looked)
 
 

time: 270 us -> 270 us (level)
  no operation moved by 1% of the time
where the time goes in v6:
time: 270 us; the launch traced here: 269 us
  blocking collectives  143 us (53%)
  waiting for transfers between devices  58.1 us (22%)
  starting transfers between devices  28.9 us (11%)
  local copies, waits for them, and re-layouts  21.7 us (8%)
  Pallas kernels  12.5 us (5%)
  other arithmetic  3.53 us (1%)
    all_to_all x1, blocking collectives, body(): lax.all_to_all(sending, 'dev', split_axis=0, concat_axis=0, tiled=True)  106 us
    all_to_all x1, waiting for transfers between devices, body(): lax.all_to_all(spread.reshape(shards * groups, per_old, piece, width), ('...  58.1 us
    all_to_all x1, blocking collectives, body(): lax.all_to_all(answer, both, split_axis=0, concat_axis=0, axis_index_grou...  37.7 us
    all_to_all x1, starting transfers between devices, body(): lax.all_to_all(spread.reshape(shards * groups, per_old, piece, width), ('...  16.7 us
    ppermute x3, starting transfers between devices, swap_groups(): lax.ppermute(part, axis, [(i, (i + by) % peers) for i in range(peers)])  12.2 us
    gather x5, local copies, waits for them, and re-layouts, body(): id_place = block_position[table_ids, lookup_ids // TILE]  9.54 us
  transfers between devices with their start and end apart: 4, of which 1 were waited for; matrix products, arithmetic and copies ran while one was open for 9% of the time, Pallas kernels for 0%

profile of v6, /device:TPU:1, one launch (start us, length us, event | category | flops | bytes accessed | tf_op | source)
XLA Modules:
  0.0 269.4 jit_solution(12342215499205294459)
XLA Ops:
  0.6 3.3 %spread_rows.1 = f32[64,4,16,2,128]{4,3,2,1,0:T(2,128)} custom-call(f32[4,16,64,2,128]{4,3,2,1,0:T(2,128)} %bitcast.117), custom_call_target="tpu_custom_call" | custom-call | tf_op jit(solution)/shard_map/spread_rows/pallas_call | solution.py:39
  3.9 16.7 %all-to-all-start = ((f32[256,16,2,128]{3,2,1,0:T(2,128)}), f32[256,16,2,128]{3,2,1,0:T(2,128)}, u32[]{:S(2)}, u32[]{:S(2)}) async-start(f32[256,16,2,128]{3,2,1,0:T(2,128)} %bitcast.116), calls=%async_computation | async-start | bytes 8388608 | tf_op jit(solution)/shard_map/all_to_all | solution.py:237
  21.0 9.1 %gather_fusion = s32[1024]{0:T(1024)S(1)} fusion(s32[4,4096]{1,0:T(4,128)S(1)} %copy-done, s32[1024]{0:T(1024)S(1)} %reshape.320), kind=kCustom, calls=%fused_computation | custom fusion | bytes 16384 | tf_op jit(solution)/shard_map/gather | solution.py:242
  31.0 2.4 reduce-window.6
  33.4 0.3 slice_reduce_fusion
  33.8 0.2 fusion.2
  34.2 0.1 copy.38
  34.4 4.3 %scatter_custom_fusion.2 = s32[2048]{0:T(1024)S(1)} fusion(s32[1024]{0:T(1024)S(1)} %reshape.358, s32[1024]{0:T(1024)S(1)} %reshape.360, s32[]{:T(128)} %constant.243.clone.1), kind=kCustom, calls=%fused_computation.110 | custom fusion | bytes 8196
  39.1 2.3 collective-permute-start.2
  41.4 4.4 %collective-permute-start.1 = (f32[20,128]{1,0:T(8,128)S(1)}, f32[20,128]{1,0:T(8,128)S(1)}, u32[]{:S(2)}, u32[]{:S(2)}) collective-permute-start(f32[20,128]{1,0:T(8,128)S(1)} %get-tuple-element.28), channel_id=1, source_target_pairs={{0,128},{64,192},{128,0},{192,64},{1,129},{65,193},{129,1},{193,65... | collective-permute-start | bytes 30728 | tf_op jit(solution)/shard_map/ppermute | solution.py:212
  45.8 5.5 %collective-permute-start = (f32[20,128]{1,0:T(8,128)S(1)}, f32[20,128]{1,0:T(8,128)S(1)}, u32[]{:S(2)}, u32[]{:S(2)}) collective-permute-start(f32[20,128]{1,0:T(8,128)S(1)} %get-tuple-element.29), channel_id=1, source_target_pairs={{0,64},{64,128},{128,192},{192,0},{1,65},{65,129},{129,193},{193,1... | collective-permute-start | bytes 30728 | tf_op jit(solution)/shard_map/ppermute | solution.py:212
  52.3 0.5 broadcast.654
  52.8 0.7 fusion.59
  53.5 0.8 gather_fusion.1
  54.5 0.2 select_reduce_fusion
  54.7 0.8 scatter_custom_fusion.1
  55.5 1.0 scatter_custom_fusion
  57.0 1.2 gather_fusion.2
  58.5 58.1 %all-to-all-done = f32[256,16,2,128]{3,2,1,0:T(2,128)} async-done(((f32[256,16,2,128]{3,2,1,0:T(2,128)}), f32[256,16,2,128]{3,2,1,0:T(2,128)}, u32[]{:S(2)}, u32[]{:S(2)}) %all-to-all-start) | async-done | bytes 4194336 | tf_op jit(solution)/shard_map/all_to_all | solution.py:237
  116.6 4.4 %place_pieces.1 = f32[4224,2,128]{2,1,0:T(2,128)S(1)} custom-call(s32[4352]{0:T(1024)S(1)} %pad_add_fusion.list_ref, f32[4096,2,128]{2,1,0:T(2,128)} %bitcast.13.in_ref, f32[20,128]{1,0:T(8,128)S(1)} %get-tuple-element.30.refs_0_, f32[20,128]{1,0:T(8,128)S(1)} %collective-permute-done.refs_1_, f32[20,128]{1,0:T(8,128)S(1)} %collective-permute-done.1.refs_2_, ...), custom_call_target="tpu_custom_call" | custom-call | tf_op jit(solution)/shard_map/place_pieces/pallas_call | solution.py:105
  121.0 105.7 %all_to_all.15.got_ref = f32[64,66,2,128]{3,2,1,0:T(2,128)S(1)} all-to-all(f32[64,66,2,128]{3,2,1,0:T(2,128)S(1)} %bitcast.111), channel_id=1, replica_groups=mesh['grp'=4,'dev'=64] {'dev'}, dimensions={0} | all-to-all | bytes 8650752 | tf_op jit(solution)/shard_map/all_to_all | solution.py:294
  226.7 2.9 %answer_and_join.1 = (f32[2048,1,128]{2,1,0:T(1,128)S(1)}, f32[64,64,2,128]{3,2,1,0:T(2,128)}, f32[64,1,128]{2,1,0:T(1,128)}) custom-call(s32[64,128]{1,0:T(8,128)S(1)} %bitcast.114, f32[8448,1,128]{2,1,0:T(1,128)S(1)} %bitcast.110, f32[64,66,2,128]{3,2,1,0:T(2,128)S(1)} %all_to_all.15.got_ref), custom_call_target="tpu_custom_call" | custom-call | tf_op jit(solution)/shard_map/answer_and_join/pallas_call | solution.py:186
  229.6 37.7 %all_to_all.16 = f32[256,8,128]{2,1,0:T(8,128)S(1)} all-to-all(f32[256,8,128]{2,1,0:T(8,128)S(1)} %bitcast.113), channel_id=1, replica_groups={{0,64,1,65,2,66,3,67,16,80,17,81,18,82,19,83,32,96,33,97,34,98,35,99,48..., dimensions={0} | all-to-all | bytes 2097152 | tf_op jit(solution)/shard_map/all_to_all | solution.py:304
  267.3 2.0 look_and_join.1
  (81 shorter events, 3.7 us)
Async XLA Ops:
  3.9 16.7 %copy-start.2 = (s32[256,4]{0,1:T(4,128)S(1)}, s32[256,4]{0,1:T(4,128)}, u32[]{:S(2)}) copy-start(s32[256,4]{0,1:T(4,128)} %param.7) | copy-start | bytes 12292
  3.9 17.0 %copy-start = (s32[4,4096]{1,0:T(4,128)S(1)}, s32[4,4096]{1,0:T(4,128)}, u32[]{:S(2)}) copy-start(s32[4,4096]{1,0:T(4,128)} %param.6) | copy-start | bytes 196612
  3.9 112.7 %all-to-all-start = ((f32[256,16,2,128]{3,2,1,0:T(2,128)}), f32[256,16,2,128]{3,2,1,0:T(2,128)}, u32[]{:S(2)}, u32[]{:S(2)}) async-start(f32[256,16,2,128]{3,2,1,0:T(2,128)} %bitcast.116), calls=%async_computation | async-start | bytes 8388608 | tf_op jit(solution)/shard_map/all_to_all | solution.py:237
  20.9 13.1 %copy-start.4 = (s32[3]{0:T(128)S(1)}, s32[3]{0:T(128)}, u32[]{:S(2)}) copy-start(s32[3]{0:T(128)} %constant.266) | copy-start | bytes 40
  20.9 13.1 %copy-start.3 = (s32[3]{0:T(128)S(1)}, s32[3]{0:T(128)}, u32[]{:S(2)}) copy-start(s32[3]{0:T(128)} %constant.269) | copy-start | bytes 40
  20.9 18.1 %copy-start.1 = (f32[4,2048]{1,0:T(4,128)S(1)}, f32[4,2048]{1,0:T(4,128)}, u32[]{:S(2)}) copy-start(f32[4,2048]{1,0:T(4,128)} %param.5) | copy-start | bytes 98308
  39.1 77.5 %collective-permute-start.2 = (f32[20,128]{1,0:T(8,128)S(1)}, f32[20,128]{1,0:T(8,128)S(1)}, u32[]{:S(2)}, u32[]{:S(2)}) collective-permute-start(f32[20,128]{1,0:T(8,128)S(1)} %get-tuple-element.27), channel_id=1, source_target_pairs={{0,192},{64,0},{128,64},{192,128},{1,193},{65,1},{129,65},{193,129... | collective-permute-start | bytes 30728 | tf_op jit(solution)/shard_map/ppermute | solution.py:212
  41.4 75.2 %collective-permute-start.1 = (f32[20,128]{1,0:T(8,128)S(1)}, f32[20,128]{1,0:T(8,128)S(1)}, u32[]{:S(2)}, u32[]{:S(2)}) collective-permute-start(f32[20,128]{1,0:T(8,128)S(1)} %get-tuple-element.28), channel_id=1, source_target_pairs={{0,128},{64,192},{128,0},{192,64},{1,129},{65,193},{129,1},{193,65... | collective-permute-start | bytes 30728 | tf_op jit(solution)/shard_map/ppermute | solution.py:212
  45.8 70.8 %collective-permute-start = (f32[20,128]{1,0:T(8,128)S(1)}, f32[20,128]{1,0:T(8,128)S(1)}, u32[]{:S(2)}, u32[]{:S(2)}) collective-permute-start(f32[20,128]{1,0:T(8,128)S(1)} %get-tuple-element.29), channel_id=1, source_target_pairs={{0,64},{64,128},{128,192},{192,0},{1,65},{65,129},{129,193},{193,1... | collective-permute-start | bytes 30728 | tf_op jit(solution)/shard_map/ppermute | solution.py:212

commit v7 on v5

--- a/solution.py
+++ b/solution.py
@@ -20,19 +20,25 @@
     piece = TILE // parts
     shape = (parts, count, blocks, piece, width)
 
+    cuts = 4
+    span = blocks // cuts
+
     def kernel(in_ref, out_ref, held, came, left):
-        def fetch(table):
-            return pltpu.make_async_copy(in_ref.at[table], held.at[table], came.at[table])
+        def fetch(table, cut):
+            some = pl.ds(cut * span, span)
+            return pltpu.make_async_copy(in_ref.at[table, some], held.at[table, some], came.at[table, cut])
 
         def table_out(table):
             return out_ref.at[:, table]
 
         for table in range(count):
-            fetch(table).start()
+            for cut in range(cuts):
+                fetch(table, cut).start()
         for table in range(count):
-            fetch(table).wait()
-            for block in range(blocks):
-                pltpu.make_async_copy(held.at[table, block], table_out(table).at[:, block], left.at[table]).start()
+            for cut in range(cuts):
+                fetch(table, cut).wait()
+                for block in range(cut * span, (cut + 1) * span):
+                    pltpu.make_async_copy(held.at[table, block], table_out(table).at[:, block], left.at[table]).start()
         for table in range(count):
             pltpu.make_async_copy(table_out(table), table_out(table), left.at[table]).wait()
 
@@ -43,7 +49,7 @@
         out_shape=jax.ShapeDtypeStruct(shape, tables.dtype),
         scratch_shapes=[
             pltpu.VMEM((count, blocks, parts, piece, width), tables.dtype),
-            pltpu.SemaphoreType.DMA((count,)),
+            pltpu.SemaphoreType.DMA((count, cuts)),
             pltpu.SemaphoreType.DMA((count,)),
         ],
         name="spread_rows",

time: 270 us -> 270 us (level)
  no operation moved by 1% of the time
where the time goes in v7:
time: 270 us
  blocking collectives  143 us (53%)
  waiting for transfers between devices  58.1 us (22%)
  starting transfers between devices  28.9 us (11%)
  local copies, waits for them, and re-layouts  21.7 us (8%)
  Pallas kernels  13 us (5%)
  other arithmetic  3.53 us (1%)
    all_to_all x1, blocking collectives, body(): lax.all_to_all(sending, 'dev', split_axis=0, concat_axis=0, tiled=True)  106 us
    all_to_all x1, waiting for transfers between devices, body(): lax.all_to_all(spread.reshape(shards * groups, per_old, piece, width), ('...  58.1 us
    all_to_all x1, blocking collectives, body(): lax.all_to_all(answer, both, split_axis=0, concat_axis=0, axis_index_grou...  37.7 us
    all_to_all x1, starting transfers between devices, body(): lax.all_to_all(spread.reshape(shards * groups, per_old, piece, width), ('...  16.7 us
    ppermute x3, starting transfers between devices, swap_groups(): lax.ppermute(part, axis, [(i, (i + by) % peers) for i in range(peers)])  12.2 us
    gather x5, local copies, waits for them, and re-layouts, body(): id_place = block_position[table_ids, lookup_ids // TILE]  9.54 us
  transfers between devices with their start and end apart: 4, of which 1 were waited for; matrix products, arithmetic and copies ran while one was open for 9% of the time, Pallas kernels for 0%

profile of v7, /device:TPU:1, one launch (start us, length us, event | category | flops | bytes accessed | tf_op | source)
XLA Modules:
  0.0 269.7 jit_solution(10605723156486536788)
XLA Ops:
  0.6 3.7 %spread_rows.1 = f32[64,4,16,2,128]{4,3,2,1,0:T(2,128)} custom-call(f32[4,16,64,2,128]{4,3,2,1,0:T(2,128)} %bitcast.117), custom_call_target="tpu_custom_call" | custom-call | tf_op jit(solution)/shard_map/spread_rows/pallas_call | solution.py:45
  4.4 16.7 %all-to-all-start = ((f32[256,16,2,128]{3,2,1,0:T(2,128)}), f32[256,16,2,128]{3,2,1,0:T(2,128)}, u32[]{:S(2)}, u32[]{:S(2)}) async-start(f32[256,16,2,128]{3,2,1,0:T(2,128)} %bitcast.116), calls=%async_computation | async-start | bytes 8388608 | tf_op jit(solution)/shard_map/all_to_all | solution.py:225
  21.4 9.1 %gather_fusion.1 = s32[1024]{0:T(1024)S(1)} fusion(s32[4,4096]{1,0:T(4,128)S(1)} %copy-done, s32[1024]{0:T(1024)S(1)} %reshape.328), kind=kCustom, calls=%fused_computation.1 | custom fusion | bytes 16384 | tf_op jit(solution)/shard_map/gather | solution.py:230
  31.5 2.4 reduce-window.6
  33.9 0.3 slice_reduce_fusion
  34.3 0.2 fusion.2
  34.7 0.1 copy.37
  34.9 4.3 %scatter_custom_fusion.2 = s32[2048]{0:T(1024)S(1)} fusion(s32[1024]{0:T(1024)S(1)} %reshape.358, s32[1024]{0:T(1024)S(1)} %reshape.360, s32[]{:T(128)} %constant.244.clone.1), kind=kCustom, calls=%fused_computation.110 | custom fusion | bytes 8196
  39.6 2.3 collective-permute-start.2
  41.9 4.4 %collective-permute-start.1 = (f32[20,128]{1,0:T(8,128)S(1)}, f32[20,128]{1,0:T(8,128)S(1)}, u32[]{:S(2)}, u32[]{:S(2)}) collective-permute-start(f32[20,128]{1,0:T(8,128)S(1)} %get-tuple-element.24), channel_id=1, source_target_pairs={{0,128},{64,192},{128,0},{192,64},{1,129},{65,193},{129,1},{193,65... | collective-permute-start | bytes 30728 | tf_op jit(solution)/shard_map/ppermute | solution.py:200
  46.3 5.5 %collective-permute-start = (f32[20,128]{1,0:T(8,128)S(1)}, f32[20,128]{1,0:T(8,128)S(1)}, u32[]{:S(2)}, u32[]{:S(2)}) collective-permute-start(f32[20,128]{1,0:T(8,128)S(1)} %get-tuple-element.25), channel_id=1, source_target_pairs={{0,64},{64,128},{128,192},{192,0},{1,65},{65,129},{129,193},{193,1... | collective-permute-start | bytes 30728 | tf_op jit(solution)/shard_map/ppermute | solution.py:200
  52.8 0.5 broadcast.654
  53.3 0.7 fusion.59
  54.0 0.8 gather_fusion
  54.9 0.2 select_reduce_fusion
  55.2 0.8 scatter_custom_fusion.1
  56.0 1.0 scatter_custom_fusion
  57.5 1.2 gather_fusion.2
  59.0 58.1 %all-to-all-done = f32[256,16,2,128]{3,2,1,0:T(2,128)} async-done(((f32[256,16,2,128]{3,2,1,0:T(2,128)}), f32[256,16,2,128]{3,2,1,0:T(2,128)}, u32[]{:S(2)}, u32[]{:S(2)}) %all-to-all-start) | async-done | bytes 4194336 | tf_op jit(solution)/shard_map/all_to_all | solution.py:225
  117.1 4.4 %place_pieces.1 = f32[4224,2,128]{2,1,0:T(2,128)S(1)} custom-call(s32[4352]{0:T(1024)S(1)} %pad_add_fusion.list_ref, f32[4096,2,128]{2,1,0:T(2,128)} %bitcast.13.in_ref, f32[20,128]{1,0:T(8,128)S(1)} %get-tuple-element.26.refs_0_, f32[20,128]{1,0:T(8,128)S(1)} %collective-permute-done.refs_1_, f32[20,128]{1,0:T(8,128)S(1)} %collective-permute-done.1.refs_2_, ...), custom_call_target="tpu_custom_call" | custom-call | tf_op jit(solution)/shard_map/place_pieces/pallas_call | solution.py:111
  121.5 105.7 %all_to_all.15.got_ref = f32[64,66,2,128]{3,2,1,0:T(2,128)S(1)} all-to-all(f32[64,66,2,128]{3,2,1,0:T(2,128)S(1)} %bitcast.111), channel_id=1, replica_groups=mesh['grp'=4,'dev'=64] {'dev'}, dimensions={0} | all-to-all | bytes 8650752 | tf_op jit(solution)/shard_map/all_to_all | solution.py:282
  227.2 2.9 %answer_and_join.1 = (f32[2048,1,128]{2,1,0:T(1,128)S(1)}, f32[64,64,2,128]{3,2,1,0:T(2,128)}, f32[64,1,128]{2,1,0:T(1,128)}) custom-call(s32[64,128]{1,0:T(8,128)S(1)} %bitcast.114, f32[8448,1,128]{2,1,0:T(1,128)S(1)} %bitcast.110, f32[64,66,2,128]{3,2,1,0:T(2,128)S(1)} %all_to_all.15.got_ref), custom_call_target="tpu_custom_call" | custom-call | tf_op jit(solution)/shard_map/answer_and_join/pallas_call | solution.py:174
  230.1 37.7 %all_to_all.16 = f32[256,8,128]{2,1,0:T(8,128)S(1)} all-to-all(f32[256,8,128]{2,1,0:T(8,128)S(1)} %bitcast.113), channel_id=1, replica_groups={{0,64,1,65,2,66,3,67,16,80,17,81,18,82,19,83,32,96,33,97,34,98,35,99,48..., dimensions={0} | all-to-all | bytes 2097152 | tf_op jit(solution)/shard_map/all_to_all | solution.py:291
  267.8 1.9 pick_rows.1
  (81 shorter events, 3.7 us)
Async XLA Ops:
  4.4 16.7 %copy-start.2 = (s32[256,4]{0,1:T(4,128)S(1)}, s32[256,4]{0,1:T(4,128)}, u32[]{:S(2)}) copy-start(s32[256,4]{0,1:T(4,128)} %param.7) | copy-start | bytes 12292
  4.4 17.0 %copy-start = (s32[4,4096]{1,0:T(4,128)S(1)}, s32[4,4096]{1,0:T(4,128)}, u32[]{:S(2)}) copy-start(s32[4,4096]{1,0:T(4,128)} %param.6) | copy-start | bytes 196612
  4.4 112.7 %all-to-all-start = ((f32[256,16,2,128]{3,2,1,0:T(2,128)}), f32[256,16,2,128]{3,2,1,0:T(2,128)}, u32[]{:S(2)}, u32[]{:S(2)}) async-start(f32[256,16,2,128]{3,2,1,0:T(2,128)} %bitcast.116), calls=%async_computation | async-start | bytes 8388608 | tf_op jit(solution)/shard_map/all_to_all | solution.py:225
  21.4 13.1 %copy-start.4 = (s32[3]{0:T(128)S(1)}, s32[3]{0:T(128)}, u32[]{:S(2)}) copy-start(s32[3]{0:T(128)} %constant.266) | copy-start | bytes 40
  21.4 13.1 %copy-start.3 = (s32[3]{0:T(128)S(1)}, s32[3]{0:T(128)}, u32[]{:S(2)}) copy-start(s32[3]{0:T(128)} %constant.269) | copy-start | bytes 40
  21.4 18.1 %copy-start.1 = (f32[4,2048]{1,0:T(4,128)S(1)}, f32[4,2048]{1,0:T(4,128)}, u32[]{:S(2)}) copy-start(f32[4,2048]{1,0:T(4,128)} %param.5) | copy-start | bytes 98308
  39.6 77.5 %collective-permute-start.2 = (f32[20,128]{1,0:T(8,128)S(1)}, f32[20,128]{1,0:T(8,128)S(1)}, u32[]{:S(2)}, u32[]{:S(2)}) collective-permute-start(f32[20,128]{1,0:T(8,128)S(1)} %get-tuple-element.23), channel_id=1, source_target_pairs={{0,192},{64,0},{128,64},{192,128},{1,193},{65,1},{129,65},{193,129... | collective-permute-start | bytes 30728 | tf_op jit(solution)/shard_map/ppermute | solution.py:200
  41.9 75.2 %collective-permute-start.1 = (f32[20,128]{1,0:T(8,128)S(1)}, f32[20,128]{1,0:T(8,128)S(1)}, u32[]{:S(2)}, u32[]{:S(2)}) collective-permute-start(f32[20,128]{1,0:T(8,128)S(1)} %get-tuple-element.24), channel_id=1, source_target_pairs={{0,128},{64,192},{128,0},{192,64},{1,129},{65,193},{129,1},{193,65... | collective-permute-start | bytes 30728 | tf_op jit(solution)/shard_map/ppermute | solution.py:200
  46.3 70.8 %collective-permute-start = (f32[20,128]{1,0:T(8,128)S(1)}, f32[20,128]{1,0:T(8,128)S(1)}, u32[]{:S(2)}, u32[]{:S(2)}) collective-permute-start(f32[20,128]{1,0:T(8,128)S(1)} %get-tuple-element.25), channel_id=1, source_target_pairs={{0,64},{64,128},{128,192},{192,0},{1,65},{65,129},{129,193},{193,1... | collective-permute-start | bytes 30728 | tf_op jit(solution)/shard_map/ppermute | solution.py:200
